TPU v7x, 128 devices: a whole 4x4x4 slice. The times are simulated.
128 devices in a mesh: row: 64 (over z, y, x), col: 2 (over core).
Axes of the slice: x: 4, y: 4, z: 4, core: 2. Of those that a mesh axis runs over, the one named last changes fastest.
Arguments:
- node_feat: bfloat16 [524288, 500], P(('row', 'col'))
- w_one: float32 [500, 256], replicated
- w_two: float32 [256, 7], replicated
- send_rows: int32 [512, 128], P(('row', 'col'))
- edge_src: int32 [524288, 6], P(('row', 'col'))
- edge_wt: float32 [524288, 6], P(('row', 'col'))
- labels: int32 [524288], P(('row', 'col'))
- label_mask: int32 [524288], P(('row', 'col'))
Outputs:
- output 1: float32 [], replicated
- output 2: float32 [500, 256], replicated
- output 3: float32 [256, 7], replicated
All inputs are finite; a program needn't handle non-finite values.
Results may differ from a plain program's by a relative error of at most 0.001.
Values are sent between devices in bfloat16 or wider.
A program may use at most 1 GiB of HBM per device.

v0:
```python
import jax
import jax.numpy as jnp
from jax import lax
from jax.sharding import PartitionSpec as P

PEERS = 4


def shift_perm(size, offset):
    return [(src_dev, (src_dev + offset) % size) for src_dev in range(size)]


def exchange(table, send_rows, n_rows, n_cols):
    outgoing = table[send_rows]
    from_left = lax.ppermute(outgoing[1], 'col', shift_perm(n_cols, 1))
    from_right = lax.ppermute(outgoing[0], 'col', shift_perm(n_cols, -1))
    from_above = lax.ppermute(outgoing[3], 'row', shift_perm(n_rows, 1))
    from_below = lax.ppermute(outgoing[2], 'row', shift_perm(n_rows, -1))
    return jnp.concatenate([table, from_left, from_right, from_above, from_below], axis=0)


def return_grads(halo_grad, n_rows, n_cols):
    for_list0 = lax.ppermute(halo_grad[1], 'col', shift_perm(n_cols, 1))
    for_list1 = lax.ppermute(halo_grad[0], 'col', shift_perm(n_cols, -1))
    for_list2 = lax.ppermute(halo_grad[3], 'row', shift_perm(n_rows, 1))
    for_list3 = lax.ppermute(halo_grad[2], 'row', shift_perm(n_rows, -1))
    return jnp.stack([for_list0, for_list1, for_list2, for_list3])


def aggregate(ext_table, src_cols, wt_cols):
    def add_edge(edge_k, total):
        return total + wt_cols[edge_k][:, None] * ext_table[src_cols[edge_k]].astype(jnp.float32)
    start_acc = jnp.zeros((src_cols.shape[1], ext_table.shape[1]), jnp.float32)
    return lax.fori_loop(0, src_cols.shape[0], add_edge, start_acc)


def scatter_back(grad, src_cols, wt_cols, ext_rows):
    def add_edge(edge_k, total):
        return total.at[src_cols[edge_k]].add(wt_cols[edge_k][:, None] * grad)
    start_acc = jnp.zeros((ext_rows, grad.shape[1]), jnp.float32)
    return lax.fori_loop(0, src_cols.shape[0], add_edge, start_acc)


def solution(mesh):
    n_rows = mesh.shape['row']
    n_cols = mesh.shape['col']
    grid_axes = ('row', 'col')

    def device_step(node_feat, w_one, w_two, send_rows, edge_src, edge_wt, labels, label_mask):
        n_local = node_feat.shape[0]
        src_cols = edge_src.T
        wt_cols = edge_wt.T
        w_one_b = w_one.astype(jnp.bfloat16)
        w_two_b = w_two.astype(jnp.bfloat16)
        ext_one = exchange(node_feat, send_rows, n_rows, n_cols)
        z_one = aggregate(ext_one, src_cols, wt_cols).astype(jnp.bfloat16)
        h_one = jnp.maximum(jnp.dot(z_one, w_one_b, preferred_element_type=jnp.float32), 0.0).astype(jnp.bfloat16)
        ext_two = exchange(h_one, send_rows, n_rows, n_cols)
        z_two = aggregate(ext_two, src_cols, wt_cols).astype(jnp.bfloat16)
        logits = jnp.dot(z_two, w_two_b, preferred_element_type=jnp.float32)
        weight = label_mask.astype(jnp.float32)
        label_count = lax.psum(jnp.sum(weight), grid_axes)
        log_norm = jax.nn.logsumexp(logits, axis=1)
        picked = jnp.take_along_axis(logits, labels[:, None], axis=1)[:, 0]
        mean_loss = lax.psum(jnp.sum(weight * (log_norm - picked)), grid_axes) / label_count
        class_prob = jnp.exp(logits - log_norm[:, None])
        onehot = (jnp.arange(logits.shape[1])[None, :] == labels[:, None]).astype(jnp.float32)
        d_logits = ((class_prob - onehot) * (weight / label_count)[:, None]).astype(jnp.bfloat16)
        grad_two = lax.psum(jnp.einsum('nf,nc->fc', z_two, d_logits, preferred_element_type=jnp.float32), grid_axes)
        d_z_two = jnp.einsum('nc,fc->nf', d_logits, w_two_b, preferred_element_type=jnp.float32)
        d_ext = scatter_back(d_z_two, src_cols, wt_cols, ext_two.shape[0])
        feat_width = d_ext.shape[1]
        halo_grad = d_ext[n_local:].reshape(PEERS, -1, feat_width)
        returned = return_grads(halo_grad, n_rows, n_cols)
        d_h_one = d_ext[:n_local].at[send_rows.reshape(-1)].add(returned.reshape(-1, feat_width))
        d_y_one = jnp.where(h_one > 0, d_h_one, 0.0).astype(jnp.bfloat16)
        grad_one = lax.psum(jnp.einsum('nf,ng->fg', z_one, d_y_one, preferred_element_type=jnp.float32), grid_axes)
        return mean_loss, grad_one, grad_two

    rows_spec = P(grid_axes, None)
    vec_spec = P(grid_axes)
    return jax.shard_map(device_step, mesh=mesh,
                         in_specs=(rows_spec, P(), P(), rows_spec, rows_spec, rows_spec, vec_spec, vec_spec),
                         out_specs=(P(), P(), P()), check_vma=False)
```

profile of v0, /device:TPU:1, one launch (start us, length us, event | category | flops | bytes accessed | tf_op | source)
XLA Modules:
  0.0 845.4 jit_solution(3929165980293603351)
XLA Ops:
  7.2 6.5 copy.14
  13.7 4.7 gather_fusion.2
  21.4 7.2 collective-permute-start.3
  28.6 4.4 constant_dynamic-update-slice_fusion.4
  35.7 177.2 %while.42 = (s32[]{:T(128)}, f32[4096,500]{1,0:T(8,128)}, f32[6,4096]{1,0:T(8,128)}, s32[6,4096]{1,0:T(8,128)}, bf16[4608,500]{1,0:T(8,128)(2,1)}, /*index=5*/s32[]{:T(128)}, s32[]{:T(128)}) while((s32[]{:T(128)}, f32[4096,500]{1,0:T(8,128)}, f32[6,4096]{1,0:T(8,128)}, s32[6,4096]{1,0:T(8,128)}, bf16[4608,500]{1,0:T(8,128)(2,1)}, ...), condition=%wide.region_1.0_spmd.clone, body=%wide.region_0.0_spmd.clone.sunk | while | flops 8208387 | bytes 28803164 | solution.py:34
  36.7 20.3 %gather_fusion = bf16[4096,500]{1,0:T(8,128)(2,1)} fusion(bf16[4608,500]{1,0:T(8,128)(2,1)} %get-tuple-element.486, s32[4096]{0:T(1024)S(1)} %broadcast_clamp_fusion.4), kind=kCustom, calls=%fused_computation.clone.clone.1 | custom fusion | bytes 8208384 | tf_op jit(solution)/shard_map/while/body/eval_jaxpr/gather | solution.py:32
  58.0 5.4 select_add_fusion.4
  64.4 20.3 %gather_fusion = bf16[4096,500]{1,0:T(8,128)(2,1)} fusion(bf16[4608,500]{1,0:T(8,128)(2,1)} %get-tuple-element.486, s32[4096]{0:T(1024)S(1)} %broadcast_clamp_fusion.4), kind=kCustom, calls=%fused_computation.clone.clone.1 | custom fusion | bytes 8208384 | tf_op jit(solution)/shard_map/while/body/eval_jaxpr/gather | solution.py:32
  85.6 7.7 select_add_fusion.4
  94.3 20.3 %gather_fusion = bf16[4096,500]{1,0:T(8,128)(2,1)} fusion(bf16[4608,500]{1,0:T(8,128)(2,1)} %get-tuple-element.486, s32[4096]{0:T(1024)S(1)} %broadcast_clamp_fusion.4), kind=kCustom, calls=%fused_computation.clone.clone.1 | custom fusion | bytes 8208384 | tf_op jit(solution)/shard_map/while/body/eval_jaxpr/gather | solution.py:32
  115.5 7.7 select_add_fusion.4
  124.2 20.3 %gather_fusion = bf16[4096,500]{1,0:T(8,128)(2,1)} fusion(bf16[4608,500]{1,0:T(8,128)(2,1)} %get-tuple-element.486, s32[4096]{0:T(1024)S(1)} %broadcast_clamp_fusion.4), kind=kCustom, calls=%fused_computation.clone.clone.1 | custom fusion | bytes 8208384 | tf_op jit(solution)/shard_map/while/body/eval_jaxpr/gather | solution.py:32
  145.4 7.7 select_add_fusion.4
  154.1 20.3 %gather_fusion = bf16[4096,500]{1,0:T(8,128)(2,1)} fusion(bf16[4608,500]{1,0:T(8,128)(2,1)} %get-tuple-element.486, s32[4096]{0:T(1024)S(1)} %broadcast_clamp_fusion.4), kind=kCustom, calls=%fused_computation.clone.clone.1 | custom fusion | bytes 8208384 | tf_op jit(solution)/shard_map/while/body/eval_jaxpr/gather | solution.py:32
  175.3 7.7 select_add_fusion.4
  184.0 20.3 %gather_fusion = bf16[4096,500]{1,0:T(8,128)(2,1)} fusion(bf16[4608,500]{1,0:T(8,128)(2,1)} %get-tuple-element.486, s32[4096]{0:T(1024)S(1)} %broadcast_clamp_fusion.4), kind=kCustom, calls=%fused_computation.clone.clone.1 | custom fusion | bytes 8208384 | tf_op jit(solution)/shard_map/while/body/eval_jaxpr/gather | solution.py:32
  205.2 7.7 select_add_fusion.4
  212.9 6.0 constant_dynamic-update-slice_fusion.9
  218.9 3.4 gather_fusion.3
  223.4 6.9 collective-permute-start.7
  232.0 138.9 %while.43 = (s32[]{:T(128)}, f32[4096,256]{1,0:T(8,128)}, f32[6,4096]{1,0:T(8,128)}, s32[6,4096]{1,0:T(8,128)}, bf16[4608,256]{1,0:T(8,128)(2,1)S(1)}, /*index=5*/s32[]{:T(128)}, s32[]{:T(128)}) while((s32[]{:T(128)}, f32[4096,256]{1,0:T(8,128)}, f32[6,4096]{1,0:T(8,128)}, s32[6,4096]{1,0:T(8,128)}, ...), condition=%wide.region_3.0_spmd.clone, body=%wide.region_2.0_spmd.clone.sunk | while | flops 4210691 | bytes 14811231 | solution.py:34
  232.9 16.9 %gather_fusion.1 = bf16[4096,256]{1,0:T(8,128)(2,1)} fusion(bf16[4608,256]{1,0:T(8,128)(2,1)S(1)} %get-tuple-element.507, s32[4096]{0:T(1024)S(1)} %broadcast_clamp_fusion.5), kind=kCustom, calls=%fused_computation.1.clone.clone.1 | custom fusion | bytes 4210688 | tf_op jit(solution)/shard_map/while/body/eval_jaxpr/gather | solution.py:32
  250.8 3.6 select_add_fusion.5
  255.3 16.9 %gather_fusion.1 = bf16[4096,256]{1,0:T(8,128)(2,1)} fusion(bf16[4608,256]{1,0:T(8,128)(2,1)S(1)} %get-tuple-element.507, s32[4096]{0:T(1024)S(1)} %broadcast_clamp_fusion.5), kind=kCustom, calls=%fused_computation.1.clone.clone.1 | custom fusion | bytes 4210688 | tf_op jit(solution)/shard_map/while/body/eval_jaxpr/gather | solution.py:32
  273.2 4.5 select_add_fusion.5
  278.6 16.9 %gather_fusion.1 = bf16[4096,256]{1,0:T(8,128)(2,1)} fusion(bf16[4608,256]{1,0:T(8,128)(2,1)S(1)} %get-tuple-element.507, s32[4096]{0:T(1024)S(1)} %broadcast_clamp_fusion.5), kind=kCustom, calls=%fused_computation.1.clone.clone.1 | custom fusion | bytes 4210688 | tf_op jit(solution)/shard_map/while/body/eval_jaxpr/gather | solution.py:32
  296.5 4.5 select_add_fusion.5
  301.9 16.9 %gather_fusion.1 = bf16[4096,256]{1,0:T(8,128)(2,1)} fusion(bf16[4608,256]{1,0:T(8,128)(2,1)S(1)} %get-tuple-element.507, s32[4096]{0:T(1024)S(1)} %broadcast_clamp_fusion.5), kind=kCustom, calls=%fused_computation.1.clone.clone.1 | custom fusion | bytes 4210688 | tf_op jit(solution)/shard_map/while/body/eval_jaxpr/gather | solution.py:32
  319.8 4.5 select_add_fusion.5
  325.2 16.9 %gather_fusion.1 = bf16[4096,256]{1,0:T(8,128)(2,1)} fusion(bf16[4608,256]{1,0:T(8,128)(2,1)S(1)} %get-tuple-element.507, s32[4096]{0:T(1024)S(1)} %broadcast_clamp_fusion.5), kind=kCustom, calls=%fused_computation.1.clone.clone.1 | custom fusion | bytes 4210688 | tf_op jit(solution)/shard_map/while/body/eval_jaxpr/gather | solution.py:32
  343.1 4.5 select_add_fusion.5
  348.5 16.9 %gather_fusion.1 = bf16[4096,256]{1,0:T(8,128)(2,1)} fusion(bf16[4608,256]{1,0:T(8,128)(2,1)S(1)} %get-tuple-element.507, s32[4096]{0:T(1024)S(1)} %broadcast_clamp_fusion.5), kind=kCustom, calls=%fused_computation.1.clone.clone.1 | custom fusion | bytes 4210688 | tf_op jit(solution)/shard_map/while/body/eval_jaxpr/gather | solution.py:32
  366.4 4.5 select_add_fusion.5
  373.8 24.5 %gather_fusion.4 = f32[4096]{0:T(1024)S(1)} fusion(f32[4096,7]{0,1:T(8,128)S(1)} %get-tuple-element.374, s32[4096]{0:T(1024)S(1)} %bitcast.45), kind=kCustom, calls=%fused_computation.4 | custom fusion | bytes 65536 | tf_op jit(solution)/shard_map/jit(take_along_axis)/gather | solution.py:64
  399.0 66.7 %psum.29 = f32[]{:T(128)} all-reduce(f32[]{:T(128)} %get-tuple-element.324), channel_id=1, replica_groups=mesh['row'=64,'col'=2] {'row','col'}, use_global_device_ids=true, to_apply=%region_9.10 | all-reduce | flops 1 | bytes 8 | tf_op jit(solution)/shard_map/psum | solution.py:62
  471.6 187.6 %while.41 = (s32[]{:T(128)}, f32[4608,256]{1,0:T(8,128)}, s32[6,4096]{1,0:T(8,128)}, f32[6,4096]{1,0:T(8,128)}, f32[4096,256]{1,0:T(8,128)}, /*index=5*/s32[]{:T(128)}) while((s32[]{:T(128)}, f32[4608,256]{1,0:T(8,128)}, s32[6,4096]{1,0:T(8,128)}, f32[6,4096]{1,0:T(8,128)}, f32[4096,256]{1,0:T(8,128)}, /*index=5*/s32[]{:T(128)}) %tuple.116), condition=%wide.region_12.13_spmd, body=%wide.region_10.0_spmd.sunk | while | flops 2109442 | bytes 8994893 | solution.py:41
  473.4 29.4 %scatter_custom_fusion.6 = f32[4608,256]{1,0:T(8,128)} fusion(f32[4608,256]{1,0:T(8,128)} %get-tuple-element.517, s32[4096]{0:T(1024)S(1)} %bitcast.54, f32[4096,256]{1,0:T(8,128)} %get-tuple-element.526, f32[4096]{0:T(1024)S(1)} %bitcast.48), kind=kCustom, calls=%fused_computation.7.clone.1 | custom fusion | flops 2097152 | bytes 8929280 | tf_op jit(solution)/shard_map/while/body/eval_jaxpr/scatter-add | solution.py:39
  504.7 29.4 %scatter_custom_fusion.6 = f32[4608,256]{1,0:T(8,128)} fusion(f32[4608,256]{1,0:T(8,128)} %get-tuple-element.517, s32[4096]{0:T(1024)S(1)} %bitcast.54, f32[4096,256]{1,0:T(8,128)} %get-tuple-element.526, f32[4096]{0:T(1024)S(1)} %bitcast.48), kind=kCustom, calls=%fused_computation.7.clone.1 | custom fusion | flops 2097152 | bytes 8929280 | tf_op jit(solution)/shard_map/while/body/eval_jaxpr/scatter-add | solution.py:39
  536.0 29.4 %scatter_custom_fusion.6 = f32[4608,256]{1,0:T(8,128)} fusion(f32[4608,256]{1,0:T(8,128)} %get-tuple-element.517, s32[4096]{0:T(1024)S(1)} %bitcast.54, f32[4096,256]{1,0:T(8,128)} %get-tuple-element.526, f32[4096]{0:T(1024)S(1)} %bitcast.48), kind=kCustom, calls=%fused_computation.7.clone.1 | custom fusion | flops 2097152 | bytes 8929280 | tf_op jit(solution)/shard_map/while/body/eval_jaxpr/scatter-add | solution.py:39
  567.2 29.4 %scatter_custom_fusion.6 = f32[4608,256]{1,0:T(8,128)} fusion(f32[4608,256]{1,0:T(8,128)} %get-tuple-element.517, s32[4096]{0:T(1024)S(1)} %bitcast.54, f32[4096,256]{1,0:T(8,128)} %get-tuple-element.526, f32[4096]{0:T(1024)S(1)} %bitcast.48), kind=kCustom, calls=%fused_computation.7.clone.1 | custom fusion | flops 2097152 | bytes 8929280 | tf_op jit(solution)/shard_map/while/body/eval_jaxpr/scatter-add | solution.py:39
  598.5 29.4 %scatter_custom_fusion.6 = f32[4608,256]{1,0:T(8,128)} fusion(f32[4608,256]{1,0:T(8,128)} %get-tuple-element.517, s32[4096]{0:T(1024)S(1)} %bitcast.54, f32[4096,256]{1,0:T(8,128)} %get-tuple-element.526, f32[4096]{0:T(1024)S(1)} %bitcast.48), kind=kCustom, calls=%fused_computation.7.clone.1 | custom fusion | flops 2097152 | bytes 8929280 | tf_op jit(solution)/shard_map/while/body/eval_jaxpr/scatter-add | solution.py:39
  629.8 29.4 %scatter_custom_fusion.6 = f32[4608,256]{1,0:T(8,128)} fusion(f32[4608,256]{1,0:T(8,128)} %get-tuple-element.517, s32[4096]{0:T(1024)S(1)} %bitcast.54, f32[4096,256]{1,0:T(8,128)} %get-tuple-element.526, f32[4096]{0:T(1024)S(1)} %bitcast.48), kind=kCustom, calls=%fused_computation.7.clone.1 | custom fusion | flops 2097152 | bytes 8929280 | tf_op jit(solution)/shard_map/while/body/eval_jaxpr/scatter-add | solution.py:39
  661.2 6.8 collective-permute-start.11
  668.0 4.4 slice.56
  672.5 7.3 scatter_fusion
  679.7 6.7 fusion.4
  689.0 65.6 %all-reduce = (f32[]{:T(128)}, f32[256,7]{0,1:T(8,128)}) all-reduce(f32[]{:T(128)} %get-tuple-element.325, f32[256,7]{0,1:T(8,128)S(1)} %fusion.9), channel_id=1, replica_groups=mesh['row'=64,'col'=2] {'row','col'}, use_global_device_ids=true, to_apply=%region_7.0 | all-reduce | flops 1793 | bytes 14344 | tf_op jit(solution)/shard_map/psum | solution.py:65
  756.0 79.6 %all-reduce.3.cloned.1.call-done = f32[500,256]{1,0:T(8,128)} async-done(((f32[500,256]{1,0:T(8,128)}), f32[500,256]{1,0:T(8,128)}) %all-reduce.3.cloned.1.call-update) | async-done | bytes 512016 | tf_op jit(solution)/shard_map/psum | solution.py:77
  (115 shorter events, 57.7 us)
Async XLA Ops:
  7.2 6.5 copy-start.5
  7.2 828.4 %all-reduce.3.cloned.1.call-start = ((), (), s32[]{:S(2)}) async-start(), calls=%async_computation | async-start | bytes 1032192 | tf_op jit(solution)/shard_map/psum | solution.py:77
  18.5 14.6 %collective-permute-start = (bf16[128,500]{1,0:T(8,128)(2,1)S(1)}, bf16[128,500]{1,0:T(8,128)(2,1)S(1)}, u32[]{:S(2)}, u32[]{:S(2)}) collective-permute-start(bf16[128,500]{1,0:T(8,128)(2,1)S(1)} %get-tuple-element.366), channel_id=1, source_target_pairs={{0,1},{1,0},{2,3},{3,2},{4,5},{5,4},{6,7},{7,6},{8,9},{9,8},{10,11... | collective-permute-start | bytes 384008 | tf_op jit(solution)/shard_map/ppermute | solution.py:15
  19.9 13.8 %collective-permute-start.1 = (bf16[128,500]{1,0:T(8,128)(2,1)S(1)}, bf16[128,500]{1,0:T(8,128)(2,1)S(1)}, u32[]{:S(2)}, u32[]{:S(2)}) collective-permute-start(bf16[128,500]{1,0:T(8,128)(2,1)S(1)} %get-tuple-element.365), channel_id=1, source_target_pairs={{0,1},{1,0},{2,3},{3,2},{4,5},{5,4},{6,7},{7,6},{8,9},{9,8},{10,11... | collective-permute-start | bytes 384008 | tf_op jit(solution)/shard_map/ppermute | solution.py:16
  20.0 14.4 %collective-permute-start.2 = (bf16[128,500]{1,0:T(8,128)(2,1)S(1)}, bf16[128,500]{1,0:T(8,128)(2,1)S(1)}, u32[]{:S(2)}, u32[]{:S(2)}) collective-permute-start(bf16[128,500]{1,0:T(8,128)(2,1)S(1)} %get-tuple-element.364), channel_id=1, source_target_pairs={{0,2},{2,4},{4,6},{6,8},{8,10},{10,12},{12,14},{14,16},{16,18},{18... | collective-permute-start | bytes 384008 | tf_op jit(solution)/shard_map/ppermute | solution.py:17
  21.4 11.6 %copy-start.2 = (s32[4096]{0:T(1024)S(1)}, s32[4096]{0:T(1024)}, u32[]{:S(2)}) copy-start(s32[4096]{0:T(1024)} %param.20) | copy-start | bytes 49156
  21.4 13.7 %collective-permute-start.3 = (bf16[128,500]{1,0:T(8,128)(2,1)S(1)}, bf16[128,500]{1,0:T(8,128)(2,1)S(1)}, u32[]{:S(2)}, u32[]{:S(2)}) collective-permute-start(bf16[128,500]{1,0:T(8,128)(2,1)S(1)} %get-tuple-element.363), channel_id=1, source_target_pairs={{0,126},{2,0},{4,2},{6,4},{8,6},{10,8},{12,10},{14,12},{16,14},{18... | collective-permute-start | bytes 384008 | tf_op jit(solution)/shard_map/ppermute | solution.py:18
  35.7 177.2 %copy-start.1 = (f32[500,256]{1,0:T(8,128)S(1)}, f32[500,256]{1,0:T(8,128)}, u32[]{:S(2)}) copy-start(f32[500,256]{1,0:T(8,128)} %param.15) | copy-start | bytes 1536004
  222.4 7.9 collective-permute-start.4
  223.2 7.1 collective-permute-start.5
  223.3 8.6 %collective-permute-start.6 = (bf16[128,256]{1,0:T(8,128)(2,1)S(1)}, bf16[128,256]{1,0:T(8,128)(2,1)S(1)}, u32[]{:S(2)}, u32[]{:S(2)}) collective-permute-start(bf16[128,256]{1,0:T(8,128)(2,1)S(1)} %get-tuple-element.368), channel_id=1, source_target_pairs={{0,2},{2,4},{4,6},{6,8},{8,10},{10,12},{12,14},{14,16},{16,18},{18... | collective-permute-start | bytes 196616 | tf_op jit(solution)/shard_map/ppermute | solution.py:17
  223.4 8.5 %collective-permute-start.7 = (bf16[128,256]{1,0:T(8,128)(2,1)S(1)}, bf16[128,256]{1,0:T(8,128)(2,1)S(1)}, u32[]{:S(2)}, u32[]{:S(2)}) collective-permute-start(bf16[128,256]{1,0:T(8,128)(2,1)S(1)} %get-tuple-element.367), channel_id=1, source_target_pairs={{0,126},{2,0},{4,2},{6,4},{8,6},{10,8},{12,10},{14,12},{16,14},{18... | collective-permute-start | bytes 196616 | tf_op jit(solution)/shard_map/ppermute | solution.py:18
  232.0 138.9 %copy-start.4 = (f32[256,7]{0,1:T(8,128)S(1)}, f32[256,7]{0,1:T(8,128)}, u32[]{:S(2)}) copy-start(f32[256,7]{0,1:T(8,128)} %param.16) | copy-start | bytes 21508
  373.8 24.5 %copy-start.3 = (s32[4096]{0:T(1024)S(1)}, s32[4096]{0:T(1024)}, u32[]{:S(2)}) copy-start(s32[4096]{0:T(1024)} %param.21) | copy-start | bytes 49156
  471.6 196.4 %copy-start.6 = (s32[4,128]{1,0:T(4,128)S(1)}, s32[4,128]{1,0:T(4,128)}, u32[]{:S(2)}) copy-start(s32[4,128]{1,0:T(4,128)} %param.17) | copy-start | bytes 6148
  660.3 12.1 %collective-permute-start.8 = (f32[128,256]{1,0:T(8,128)S(1)}, f32[128,256]{1,0:T(8,128)S(1)}, u32[]{:S(2)}, u32[]{:S(2)}) collective-permute-start(f32[128,256]{1,0:T(8,128)S(1)} %get-tuple-element.359), channel_id=1, source_target_pairs={{0,1},{1,0},{2,3},{3,2},{4,5},{5,4},{6,7},{7,6},{8,9},{9,8},{10,11... | collective-permute-start | bytes 393224 | tf_op jit(solution)/shard_map/ppermute | solution.py:23
  661.0 11.4 %collective-permute-start.9 = (f32[128,256]{1,0:T(8,128)S(1)}, f32[128,256]{1,0:T(8,128)S(1)}, u32[]{:S(2)}, u32[]{:S(2)}) collective-permute-start(f32[128,256]{1,0:T(8,128)S(1)} %get-tuple-element.362), channel_id=1, source_target_pairs={{0,1},{1,0},{2,3},{3,2},{4,5},{5,4},{6,7},{7,6},{8,9},{9,8},{10,11... | collective-permute-start | bytes 393224 | tf_op jit(solution)/shard_map/ppermute | solution.py:24
  661.1 11.3 %collective-permute-start.10 = (f32[128,256]{1,0:T(8,128)S(1)}, f32[128,256]{1,0:T(8,128)S(1)}, u32[]{:S(2)}, u32[]{:S(2)}) collective-permute-start(f32[128,256]{1,0:T(8,128)S(1)} %get-tuple-element.361), channel_id=1, source_target_pairs={{0,2},{2,4},{4,6},{6,8},{8,10},{10,12},{12,14},{14,16},{16,18},{18... | collective-permute-start | bytes 393224 | tf_op jit(solution)/shard_map/ppermute | solution.py:25
  661.2 11.2 %collective-permute-start.11 = (f32[128,256]{1,0:T(8,128)S(1)}, f32[128,256]{1,0:T(8,128)S(1)}, u32[]{:S(2)}, u32[]{:S(2)}) collective-permute-start(f32[128,256]{1,0:T(8,128)S(1)} %get-tuple-element.360), channel_id=1, source_target_pairs={{0,126},{2,0},{4,2},{6,4},{8,6},{10,8},{12,10},{14,12},{16,14},{18... | collective-permute-start | bytes 393224 | tf_op jit(solution)/shard_map/ppermute | solution.py:26
  672.5 7.3 copy-start
Sparse Core Ops, SparseCore 0:
  686.5 148.9 all-reduce.2
where the time goes:
time: 847 us; the launch traced here: 845 us
  local copies, waits for them, and re-layouts  296 us (35%)
  other arithmetic  272 us (32%)
  blocking collectives  132 us (16%)
  waiting for transfers between devices  81.2 us (10%)
  starting transfers between devices  25.7 us (3%)
  matrix products  20.8 us (2%)
  between operations  16.8 us (2%)
    gather x12, local copies, waits for them, and re-layouts, add_edge(): ext_table[src_cols[edge_k]].astype(jnp.float32)  224 us
    scatter-add x6, other arithmetic, add_edge(): return total.at[src_cols[edge_k]].add(wt_cols[edge_k][:, None] * grad)  176 us
    psum x1, waiting for transfers between devices, device_step(): lax.psum(jnp.einsum('nf,ng->fg', z_one, d_y_one, preferred_element_type=j...  79.6 us
    add x12, other arithmetic, add_edge(): total + wt_cols[edge_k][:, None] * ext_table[src_cols[edge_k]].astype(jnp...  69.9 us
    psum x1, blocking collectives, device_step(): label_count = lax.psum(jnp.sum(weight), grid_axes)  66.7 us
    psum x1, blocking collectives, device_step(): lax.psum(jnp.sum(weight * (log_norm - picked)), grid_axes) / label_count  65.6 us
    gather x1, local copies, waits for them, and re-layouts, device_step(): picked = jnp.take_along_axis(logits, labels[:, None], axis=1)[:, 0]  24.5 us
  transfers between devices with their start and end apart: 13, of which 2 were waited for; matrix products, arithmetic and copies ran while one was open for 2% of the time, Pallas kernels for 0%

commit v1 on v0

v1 whole, which is shorter than its diff:
```python
import functools

import jax
import jax.numpy as jnp
from jax import lax
from jax.experimental import pallas as pl
from jax.experimental.pallas import tpu as pltpu
from jax.sharding import PartitionSpec as P

MESH = pl.DeviceIdType.MESH
PEERS = 4
LANES = 128
BLOCK = 256
AR_ROWS = 1024
NT = (((1,), (1,)), ((), ()))
TN = (((0,), (0,)), ((), ()))
F32 = jnp.float32
BF16 = jnp.bfloat16
VMEM = pl.BlockSpec(memory_space=pltpu.VMEM)
SMEM = pl.BlockSpec(memory_space=pltpu.SMEM)


def row_digits(n_rows):
    digits, stride = [], 1
    while stride < n_rows:
        size = min(4, n_rows // stride)
        digits.append((size, stride))
        stride *= size
    return digits


def pieces(value):
    first = value.astype(BF16)
    rest = value - first.astype(F32)
    second = rest.astype(BF16)
    return [first, second, (rest - second.astype(F32)).astype(BF16)]


def iota(shape, dim):
    return lax.broadcasted_iota(jnp.int32, shape, dim)


def block_of_unit(shape):
    return lax.shift_right_logical(iota(shape, 0) * 9363, 16)


def spread_classes(n_class):
    unit = iota((LANES, 8), 0)
    return ((unit - block_of_unit((LANES, 8)) * n_class) == iota((LANES, 8), 1)).astype(F32).astype(BF16)


def block_rows(blk):
    return pl.ds(pl.multiple_of(blk * BLOCK, BLOCK), BLOCK)


def remote(src, dst, send, recv, dev):
    return pltpu.make_async_remote_copy(src_ref=src, dst_ref=dst, send_sem=send, recv_sem=recv,
                                        device_id=dev, device_id_type=MESH)


def finish(copies):
    for copy in copies:
        copy.wait_recv()
    for copy in copies:
        copy.wait_send()


def grid_peers(n_rows, n_cols):
    row, col = lax.axis_index('row'), lax.axis_index('col')
    return [(row, lax.rem(col + n_cols - 1, n_cols)), (row, lax.rem(col + 1, n_cols)),
            (lax.rem(row + n_rows - 1, n_rows), col), (lax.rem(row + 1, n_rows), col)]


def torus_axes(n_rows, n_cols):
    row, col = lax.axis_index('row'), lax.axis_index('col')
    axes = [(n_cols, col, lambda d: (row, lax.rem(col + d, n_cols)))]
    for size, stride in row_digits(n_rows):
        place = lax.rem(row // stride, size)
        axes.append((size, place, functools.partial(
            lambda d, size, stride, place: (row + (lax.rem(place + d, size) - place) * stride, col),
            size=size, stride=stride, place=place)))
    return axes


def meet(devices):
    barrier = pltpu.get_barrier_semaphore()
    for dev in devices:
        pl.semaphore_signal(barrier, inc=1, device_id=dev, device_id_type=MESH)
    pl.semaphore_wait(barrier, len(devices))


def start_exchange(peers, sbuf, rbuf, send_sem, recv_sem):
    copies = [remote(sbuf.at[q], rbuf.at[q ^ 1], send_sem.at[q], recv_sem.at[q ^ 1], peers[q]) for q in range(PEERS)]
    for copy in copies:
        copy.start()
    return copies


def exchange_kernel(n_rows, n_cols, sbuf, rbuf, send_sem, recv_sem):
    peers = grid_peers(n_rows, n_cols)
    meet(peers)
    finish(start_exchange(peers, sbuf, rbuf, send_sem, recv_sem))


def exchange_count_kernel(n_rows, n_cols, sbuf, count, rbuf, total_out, cv, cr, send_sem, recv_sem, c_send, c_recv):
    peers, axes = grid_peers(n_rows, n_cols), torus_axes(n_rows, n_cols)
    meet(peers + [dev(d) for size, _, dev in axes for d in range(1, size)])
    copies = start_exchange(peers, sbuf, rbuf, send_sem, recv_sem)
    for i, (size, _, dev) in enumerate(axes):
        held = count if i == 0 else cv.at[i - 1]
        counts = [remote(held, cr.at[i, d - 1], c_send.at[i, d - 1], c_recv.at[i, d - 1], dev(d))
                  for d in range(1, size)]
        for copy in counts:
            copy.start()
        finish(counts)
        total = held[...]
        for d in range(1, size):
            total = total + cr[i, d - 1]
        cv[i] = total
    total_out[...] = cv[len(axes) - 1]
    finish(copies)


def reduce_kernel(n_rows, n_cols, n_feat, n_class, ar, count, g1_out, g2_out, loss_out, part, gb, rs,
                  r_send, r_recv, g_send, g_recv):
    axes = torus_axes(n_rows, n_cols)
    meet([dev(d) for size, _, dev in axes for d in range(1, size)])
    length, base, spans, at, offset, held = AR_ROWS, 0, [], 0, 0, ar
    for i, (size, place, dev) in enumerate(axes):
        length //= size
        copies = []
        for d in range(1, size):
            there = pl.multiple_of(lax.rem(place + d, size) * length, 8)
            copies.append(remote(held.at[pl.ds(there, length), :], rs.at[pl.ds(at + (d - 1) * length, length), :],
                                 r_send.at[i, d - 1], r_recv.at[i, d - 1], dev(d)))
        for copy in copies:
            copy.start()
        finish(copies)
        total = held[pl.ds(pl.multiple_of(place * length, 8), length), :]
        for d in range(1, size):
            total = total + rs[at + (d - 1) * length:at + d * length, :]
        part[offset:offset + length, :] = total
        held = part.at[pl.ds(offset, length), :]
        base = pl.multiple_of(base + place * length, 8)
        at += (size - 1) * length
        offset += length
        spans.append((base, length))
    gb[pl.ds(base, length), :] = held[...]
    for i in reversed(range(len(axes))):
        size, _, dev = axes[i]
        base, length = spans[i]
        here = gb.at[pl.ds(base, length), :]
        copies = [remote(here, here, g_send.at[i, d - 1], g_recv.at[i, d - 1], dev(d)) for d in range(1, size)]
        for copy in copies:
            copy.start()
        finish(copies)
    half = AR_ROWS // 2
    for j in range(2):
        lanes = slice(j * LANES, (j + 1) * LANES)
        g1_out[:, lanes] = gb[j * half:j * half + n_feat, :]
        g2_out[:, lanes] = gb[j * half + n_feat:j * half + n_feat + n_class, :]
    loss_out[...] = gb[n_feat + n_class:n_feat + n_class + 1, :] / count[0:1, :]


def send_kernel(xt, send_v, msk, sbuf, count):
    n_feat, n_local = xt.shape
    wide = sbuf.shape[1]
    count[...] = jnp.full(count.shape, jnp.sum(msk[...].astype(F32)), F32)
    for q in range(PEERS):
        dst = send_v[q:q + 1, :]

        def pick(blk, total):
            hot = (iota((BLOCK, wide), 0) + blk * BLOCK == dst).astype(F32).astype(BF16)
            return total + lax.dot_general(hot, xt[:, block_rows(blk)], (((0,), (1,)), ((), ())),
                                           preferred_element_type=F32)

        rows = lax.fori_loop(0, n_local // BLOCK, pick, jnp.zeros((wide, n_feat), F32)).astype(BF16)
        sbuf[q, :, 0:n_feat] = rows
        sbuf[q, :, n_feat:] = jnp.zeros((wide, sbuf.shape[2] - n_feat), BF16)


def spread_weights(wt_v, wb):
    def spread(blk, _):
        at = pl.ds(pl.multiple_of(blk * LANES, LANES), LANES)
        for k in range(wt_v.shape[0]):
            wb[k, at, :] = jnp.transpose(jnp.broadcast_to(wt_v[k:k + 1, at], (LANES, LANES)))
        return 0

    lax.fori_loop(0, wt_v.shape[1] // LANES, spread, 0)


def store_halo(table, n_local, rbuf):
    halo = rbuf.shape[1]
    for p in range(PEERS):
        for j in range(rbuf.shape[2] // LANES):
            table[pl.ds((n_local + p * halo) * 4 + j, halo, stride=4), :] = (
                rbuf[p, :, j * LANES:(j + 1) * LANES].astype(F32))


def gather_block(table, parts, src_s, wb, zb, blk):
    degree, n_local, _ = wb.shape

    def some(i, _):
        base = blk * BLOCK + i * 16
        for s in range(16):
            total = None
            for k in range(degree):
                at = pl.multiple_of(src_s[k * n_local + base + s], 4)
                term = table[pl.ds(at, parts), :] * jnp.broadcast_to(wb[k, pl.ds(base + s, 1), :], (parts, LANES))
                total = term if total is None else total + term
            zb[pl.ds(pl.multiple_of((i * 16 + s) * parts, parts), parts), :] = total
        return 0

    lax.fori_loop(0, BLOCK // 16, some, 0)
    return jnp.concatenate([zb[pl.ds(j, BLOCK, stride=parts), :] for j in range(parts)], axis=1).astype(BF16)


def layer_one_kernel(src_s, send_s, xt, wt_v, rbuf, w1, z1, h1, sbuf, tab, tab2, wb, zb, w1b):
    n_feat, n_local = xt.shape
    n_blocks = n_local // BLOCK
    halo = sbuf.shape[1]
    eye = (iota((BLOCK, BLOCK), 0) == iota((BLOCK, BLOCK), 1)).astype(F32).astype(BF16)

    def fill_table(blk, _):
        rows = lax.dot_general(eye, xt[:, block_rows(blk)], NT, preferred_element_type=F32)
        for j in range(4):
            part = rows[:, j * LANES:(j + 1) * LANES]
            if part.shape[1] < LANES:
                part = jnp.concatenate([part, jnp.zeros((BLOCK, LANES - part.shape[1]), F32)], axis=1)
            tab[pl.ds(blk * (4 * BLOCK) + j, BLOCK, stride=4), :] = part
        return 0

    lax.fori_loop(0, n_blocks, fill_table, 0)
    spread_weights(wt_v, wb)
    w1b[...] = jnp.zeros(w1b.shape, BF16)
    w1b[0:n_feat, :] = w1[...].astype(BF16)
    store_halo(tab, n_local, rbuf)

    def layer_one(blk, _):
        rows = block_rows(blk)
        z = gather_block(tab, 4, src_s, wb, zb, blk)
        z1[rows, :] = z
        h = jnp.maximum(jnp.dot(z, w1b[...], preferred_element_type=F32), 0.0).astype(BF16)
        h1[rows, :] = h
        for j in range(2):
            tab2[pl.ds(blk * (2 * BLOCK) + j, BLOCK, stride=2), :] = h[:, j * LANES:(j + 1) * LANES].astype(F32)
        return 0

    lax.fori_loop(0, n_blocks, layer_one, 0)

    for q in range(PEERS):
        def take(i, _):
            for s in range(16):
                r = i * 16 + s
                at = pl.multiple_of(send_s[q * halo + r], 2)
                zb[pl.ds(pl.multiple_of(r * 2, 2), 2), :] = tab2[pl.ds(at, 2), :]
            return 0
        lax.fori_loop(0, halo // 16, take, 0)
        for j in range(2):
            sbuf[q, :, j * LANES:(j + 1) * LANES] = zb[pl.ds(j, halo, stride=2), :].astype(BF16)


def layer_two_kernel(src_s, src_v, wt_v, lab, msk, count, h1, rbuf, w2t, acc, hs, g2t, loss,
                     tab, wb, zb, z2, lg):
    degree, n_local = src_v.shape
    n_class = w2t.shape[0]
    n_blocks = n_local // BLOCK
    halo = rbuf.shape[1]

    def fill_table(blk, _):
        rows = h1[block_rows(blk), :].astype(F32)
        for j in range(2):
            tab[pl.ds(blk * (4 * BLOCK) + j, BLOCK, stride=4), :] = rows[:, j * LANES:(j + 1) * LANES]
        return 0

    lax.fori_loop(0, n_blocks, fill_table, 0)
    spread_weights(wt_v, wb)
    store_halo(tab, n_local, rbuf)
    w2p = jnp.concatenate([w2t[...], jnp.zeros((8 - n_class, w2t.shape[1]), F32)], axis=0).astype(BF16)

    def layer_two(blk, _):
        rows = block_rows(blk)
        z = gather_block(tab, 2, src_s, wb, zb, blk)
        z2[rows, :] = z
        lg[:, rows] = lax.dot_general(w2p, z, NT, preferred_element_type=F32)
        return 0

    lax.fori_loop(0, n_blocks, layer_two, 0)

    logits = lg[...]
    cls = iota(logits.shape, 0)
    real = cls < n_class
    top = jnp.max(jnp.where(real, logits, jnp.finfo(F32).min), axis=0, keepdims=True)
    log_norm = top + jnp.log(jnp.sum(jnp.where(real, jnp.exp(logits - top), 0.0), axis=0, keepdims=True))
    onehot = (cls == lab[...]).astype(F32)
    picked = jnp.sum(onehot * logits, axis=0, keepdims=True)
    weight = msk[...].astype(F32)
    loss[...] = jnp.broadcast_to(jnp.sum(weight * (log_norm - picked), axis=1, keepdims=True), loss.shape)
    prob = jnp.where(real, jnp.exp(logits - log_norm), 0.0)
    lg[...] = (prob - onehot) * (weight / count[0:1, 0:1])

    spread_cls = spread_classes(n_class)
    lc_blk = block_of_unit((LANES, BLOCK))
    slot = iota((BLOCK, BLOCK), 0)
    acc[...] = jnp.zeros(acc.shape, F32)
    g2t[...] = jnp.zeros(g2t.shape, F32)

    def scatter(blk, _):
        cols = block_rows(blk)
        g = lg[:, cols].astype(BF16)
        g2t[...] += jnp.dot(g, z2[cols, :], preferred_element_type=F32)
        tiled = jnp.dot(spread_cls, g, preferred_element_type=F32)
        total = acc[...]
        for k in range(degree):
            src = src_v[k:k + 1, cols]
            left = jnp.where(lax.shift_right_logical(src, 8) == lc_blk, tiled, 0.0).astype(BF16)
            here = (src & (BLOCK - 1)) == slot
            for part in pieces(wt_v[k:k + 1, cols]):
                right = jnp.where(here, part.astype(F32), 0.0).astype(BF16)
                total = total + lax.dot_general(left, right, NT, preferred_element_type=F32)
        acc[...] = total
        return 0

    lax.fori_loop(0, n_blocks, scatter, 0)

    hs[...] = jnp.zeros(hs.shape, F32)
    for p in range(PEERS):
        first = (n_local + p * halo) // BLOCK * n_class
        lane = (n_local + p * halo) % BLOCK
        hs[p, 0:n_class, :] = acc[first:first + n_class, lane:lane + halo]


def weight_grad_kernel(acc, hr, send_v, z1, h1, w2t, g2t, loss, ar):
    n_class = w2t.shape[0]
    n_local = h1.shape[0]
    n_feat = AR_ROWS // 2 - 12
    spread_cls = spread_classes(n_class)
    w2p = jnp.concatenate([w2t[...], jnp.zeros((8 - n_class, w2t.shape[1]), F32)], axis=0).astype(BF16)
    returned = jnp.concatenate([hr[q] for q in range(PEERS)], axis=1)
    dst = send_v[...]
    wide = dst.shape[1]
    dst_blk = lax.shift_right_logical(dst, 8) == block_of_unit((LANES, wide))
    right = ((dst & (BLOCK - 1)) == iota((BLOCK, wide), 0)).astype(F32).astype(BF16)
    total = acc[...]
    for part in pieces(returned):
        tiled = jnp.dot(spread_cls, part, preferred_element_type=F32)
        left = jnp.where(dst_blk, tiled, 0.0).astype(BF16)
        total = total + lax.dot_general(left, right, NT, preferred_element_type=F32)
    turned = jnp.concatenate(pieces(jnp.transpose(total)), axis=1)

    w2_tiled = jnp.dot(spread_cls, w2p, preferred_element_type=F32)
    lc_blk = block_of_unit((LANES, w2t.shape[1]))
    ar[...] = jnp.zeros(ar.shape, F32)
    half = AR_ROWS // 2

    def weight_grad(blk, _):
        rows = block_rows(blk)
        w2_here = jnp.where(lc_blk == blk, w2_tiled, 0.0).astype(BF16)
        dh = jnp.dot(turned, jnp.concatenate([w2_here] * 3, axis=0), preferred_element_type=F32)
        d_one = jnp.where(h1[rows, :].astype(F32) > 0, dh, 0.0).astype(BF16)
        grad = lax.dot_general(z1[rows, :], d_one, TN, preferred_element_type=F32)
        ar[0:half, :] += grad[:, :LANES]
        ar[half:2 * half, :] += grad[:, LANES:]
        return 0

    lax.fori_loop(0, n_local // BLOCK, weight_grad, 0)
    for j in range(2):
        ar[j * half + n_feat:j * half + n_feat + n_class, :] = g2t[0:n_class, j * LANES:(j + 1) * LANES]
    ar[n_feat + n_class:n_feat + n_class + 1, :] = loss[0:1, :]


def call(kernel, name, outs, in_specs, scratch, args, collective=None):
    params = dict(vmem_limit_bytes=60 * 1024 * 1024)
    if collective is not None:
        params = dict(collective_id=collective, has_side_effects=True)
    shapes = tuple(jax.ShapeDtypeStruct(*o) for o in outs)
    return pl.pallas_call(kernel, out_shape=shapes, in_specs=in_specs, out_specs=(VMEM,) * len(outs),
                          scratch_shapes=scratch, compiler_params=pltpu.CompilerParams(**params), name=name)(*args)


def solution(mesh):
    n_rows = mesh.shape['row']
    n_cols = mesh.shape['col']
    grid_axes = ('row', 'col')

    def device_step(node_feat, w_one, w_two, send_rows, edge_src, edge_wt, labels, label_mask):
        n_local, n_feat = node_feat.shape
        hidden, n_class = w_two.shape
        halo = send_rows.shape[1]
        degree = edge_src.shape[1]
        ext = n_local + PEERS * halo
        sizes = [n_cols] + [s for s, _ in row_digits(n_rows)]
        n_axes = len(sizes)
        dma, vm = pltpu.SemaphoreType.DMA, pltpu.VMEM
        feat_pad = 4 * LANES
        xt, src_v, wt_v, w2t = node_feat.T, edge_src.T, edge_wt.T, w_two.T
        src_s = (src_v * 4).reshape(-1)
        lab, msk = labels.reshape(1, -1), label_mask.reshape(1, -1)

        sbuf, count = call(send_kernel, 'send', [((PEERS, halo, feat_pad), BF16), ((8, LANES), F32)],
                           [VMEM] * 3, [], (xt, send_rows, msk))
        rbuf, count = call(
            functools.partial(exchange_count_kernel, n_rows, n_cols), 'exchange_count',
            [((PEERS, halo, feat_pad), BF16), ((8, LANES), F32)], [VMEM] * 2,
            [vm((n_axes, 8, LANES), F32), vm((n_axes, 3, 8, LANES), F32),
             dma((PEERS,)), dma((PEERS,)), dma((n_axes, 3)), dma((n_axes, 3))], (sbuf, count), 0)
        z1, h1, sbuf2 = call(
            layer_one_kernel, 'layer_one',
            [((n_local, feat_pad), BF16), ((n_local, hidden), BF16), ((PEERS, halo, hidden), BF16)],
            [SMEM] * 2 + [VMEM] * 4,
            [vm((ext * 4, LANES), F32), vm((n_local * 2, LANES), F32), vm((degree, n_local, LANES), F32),
             vm((BLOCK * 4, LANES), F32), vm((feat_pad, hidden), BF16)],
            (src_s, (send_rows * 2).reshape(-1), xt, wt_v, rbuf, w_one))
        rbuf2, = call(functools.partial(exchange_kernel, n_rows, n_cols), 'exchange_hidden',
                      [((PEERS, halo, hidden), BF16)], [VMEM], [dma((PEERS,)), dma((PEERS,))], (sbuf2,), 1)
        acc, hs, g2t, loss = call(
            layer_two_kernel, 'layer_two',
            [((LANES, BLOCK), F32), ((PEERS, 8, halo), F32), ((8, hidden), F32), ((8, LANES), F32)],
            [SMEM] + [VMEM] * 8,
            [vm((ext * 4, LANES), F32), vm((degree, n_local, LANES), F32), vm((BLOCK * 2, LANES), F32),
             vm((n_local, hidden), BF16), vm((8, n_local), F32)],
            (src_s, src_v, wt_v, lab, msk, count, h1, rbuf2, w2t))
        hr, = call(functools.partial(exchange_kernel, n_rows, n_cols), 'exchange_grad',
                   [((PEERS, 8, halo), F32)], [VMEM], [dma((PEERS,)), dma((PEERS,))], (hs,), 2)
        ar, = call(weight_grad_kernel, 'weight_grad', [((AR_ROWS, LANES), F32)], [VMEM] * 8, [],
                   (acc, hr, send_rows.reshape(1, -1), z1, h1, w2t, g2t, loss))
        part_rows, rs_rows, left = 0, 0, AR_ROWS
        for size in sizes:
            left //= size
            part_rows += left
            rs_rows += (size - 1) * left
        g1, g2, total = call(
            functools.partial(reduce_kernel, n_rows, n_cols, n_feat, n_class), 'reduce',
            [((n_feat, hidden), F32), ((n_class, hidden), F32), ((1, LANES), F32)], [VMEM] * 2,
            [vm((part_rows, LANES), F32), vm((AR_ROWS, LANES), F32), vm((rs_rows, LANES), F32),
             dma((n_axes, 3)), dma((n_axes, 3)), dma((n_axes, 3)), dma((n_axes, 3))], (ar, count), 3)
        return total[0, 0], g1, g2.T

    rows_spec = P(grid_axes, None)
    vec_spec = P(grid_axes)
    return jax.shard_map(device_step, mesh=mesh,
                         in_specs=(rows_spec, P(), P(), rows_spec, rows_spec, rows_spec, vec_spec, vec_spec),
                         out_specs=(P(), P(), P()), check_vma=False)
```

time: 847 us -> 208 us (0.25)
  local copies, waits for them, and re-layouts: 296 us -> 3.86 us
  other arithmetic: 272 us -> 2.18 us
  Pallas kernels: 0 us -> 199 us
  blocking collectives: 132 us -> 0 us
  waiting for transfers between devices: 81.2 us -> 0 us
  starting transfers between devices: 25.7 us -> 0 us
  matrix products: 20.8 us -> 0 us
  between operations: 16.8 us -> 2.41 us
    gather x15 -> x0, local copies, waits for them, and re-layouts: 256 us -> none  [the longest x12 224 us: add_edge(): ext_table[src_cols[edge_k]].astype(jnp.float32)]
    pallas_call x0 -> x8, Pallas kernels: none -> 199 us  [call(): pl.pallas_call(kernel, out_shape=shapes, in_specs=in_specs, out_specs=(VM...]
    scatter-add x7 -> x0, other arithmetic: 184 us -> none  [the longest x6 176 us: add_edge(): return total.at[src_cols[edge_k]].add(wt_cols[edge_k][:, None] * grad)]
    psum x2 -> x0, blocking collectives: 132 us -> none  [the longest x1 66.7 us: device_step(): label_count = lax.psum(jnp.sum(weight), grid_axes)]
    psum x1 -> x0, waiting for transfers between devices: 79.6 us -> none  [device_step(): lax.psum(jnp.einsum('nf,ng->fg', z_one, d_y_one, preferred_element_type=j...]
    add x12 -> x0, other arithmetic: 69.9 us -> none  [add_edge(): total + wt_cols[edge_k][:, None] * ext_table[src_cols[edge_k]].astype(jnp...]
    ppermute x12 -> x0, starting transfers between devices: 25.6 us -> none  [the longest x2 14.1 us: exchange(): from_below = lax.ppermute(outgoing[2], 'row', shift_perm(n_rows, -1))]
    dot_general x5 -> x0, matrix products: 20.8 us -> none  [the longest x1 6.67 us: device_step(): jnp.einsum('nf,ng->fg', z_one, d_y_one, preferred_element_type=jnp.float32)]
  transfers between devices with their start and end apart: 13 -> 0, of which waited for: 2 -> 0; matrix products, arithmetic and copies ran while one was open for 2% -> 0% of each run, Pallas kernels for 0% -> 0%
where the time goes in v1:
time: 208 us; the launch traced here: 207 us
  Pallas kernels  199 us (96%)
  local copies, waits for them, and re-layouts  3.86 us (2%)
  between operations  2.41 us (1%)
  other arithmetic  2.18 us (1%)
    pallas_call x8, Pallas kernels, call(): pl.pallas_call(kernel, out_shape=shapes, in_specs=in_specs, out_specs=(VM...  199 us

profile of v1, /device:TPU:1, one launch (start us, length us, event | category | flops | bytes accessed | tf_op | source)
XLA Modules:
  0.0 207.3 jit_solution(13515644730391159829)
XLA Ops:
  0.6 1.3 multiply_bitcast_fusion.send_s
  1.9 0.9 broadcast_multiply_fusion
  2.8 0.7 reshape.21.src_s
  3.5 19.0 %send.1 = (bf16[4,128,512]{2,1,0:T(8,128)(2,1)}, f32[8,128]{1,0:T(8,128)}) custom-call(bf16[500,4096]{1,0:T(8,128)(2,1)} %bitcast.13, s32[4,128]{1,0:T(4,128)} %send_v.1, s32[1,4096]{1,0:T(1,128)} %bitcast.18), custom_call_target="tpu_custom_call" | custom-call | tf_op jit(solution)/shard_map/send/pallas_call | solution.py:377
  22.5 19.4 %exchange_count.1 = (bf16[4,128,512]{2,1,0:T(8,128)(2,1)}, f32[8,128]{1,0:T(8,128)}) custom-call(bf16[4,128,512]{2,1,0:T(8,128)(2,1)} %get-tuple-element.17.sbuf, f32[8,128]{1,0:T(8,128)} %get-tuple-element.18.count), custom_call_target="tpu_custom_call" | custom-call | tf_op jit(solution)/shard_map/exchange_count/pallas_call | solution.py:377
  41.9 41.3 %layer_one.1 = (bf16[4096,512]{1,0:T(8,128)(2,1)}, bf16[4096,256]{1,0:T(8,128)(2,1)}, bf16[4,128,256]{2,1,0:T(8,128)(2,1)}) custom-call(s32[24576]{0:T(1024)} %reshape.21.src_s, s32[512]{0:T(512)} %multiply_bitcast_fusion.send_s, bf16[500,4096]{1,0:T(8,128)(2,1)} %bitcast.14, f32[6,4096]{1,0:T(8,128)} %bitcast.15, ...), custom_call_target="tpu_custom_call" | custom-call | tf_op jit(solution)/shard_map/layer_one/pallas_call | solution.py:377
  83.2 11.8 %exchange_hidden.1.rbuf = bf16[4,128,256]{2,1,0:T(8,128)(2,1)} custom-call(bf16[4,128,256]{2,1,0:T(8,128)(2,1)} %get-tuple-element.22.sbuf), custom_call_target="tpu_custom_call" | custom-call | tf_op jit(solution)/shard_map/exchange_hidden/pallas_call | solution.py:377
  95.0 49.0 %layer_two.1 = (f32[128,256]{1,0:T(8,128)}, f32[4,8,128]{2,1,0:T(8,128)}, f32[8,256]{1,0:T(8,128)}, f32[8,128]{1,0:T(8,128)}) custom-call(s32[24576]{0:T(1024)} %reshape.21.src_s, s32[6,4096]{1,0:T(8,128)} %bitcast.17, f32[6,4096]{1,0:T(8,128)} %bitcast.16, s32[1,4096]{1,0:T(1,128)} %bitcast.23, s32[1,4096]{1,0:T(1,128)} %bitcast.19, ...), custom_call_target="tpu_custom_call" | custom-call | tf_op jit(solution)/shard_map/layer_two/pallas_call | solution.py:377
  144.0 10.4 %exchange_grad.1.hr = f32[4,8,128]{2,1,0:T(8,128)} custom-call(f32[4,8,128]{2,1,0:T(8,128)} %get-tuple-element.24.sbuf), custom_call_target="tpu_custom_call" | custom-call | tf_op jit(solution)/shard_map/exchange_grad/pallas_call | solution.py:377
  154.5 13.2 %weight_grad.1.ar = f32[1024,128]{1,0:T(8,128)} custom-call(f32[128,256]{1,0:T(8,128)} %get-tuple-element.23.acc, f32[4,8,128]{2,1,0:T(8,128)} %exchange_grad.1.hr, s32[1,512]{1,0:T(1,128)} %bitcast.22, bf16[4096,512]{1,0:T(8,128)(2,1)} %get-tuple-element.25.z1, bf16[4096,256]{1,0:T(8,128)(2,1)} %get-tuple-element.21.h1, f32[7,256]{1,0:T(8,128)} %bitcast.21, ...), custom_call_target="tpu_custom_call" | custom-call | tf_op jit(solution)/shard_map/weight_grad/pallas_call | solution.py:377
  167.6 34.7 %reduce.1 = (f32[500,256]{1,0:T(8,128)}, f32[7,256]{1,0:T(8,128)}, f32[1,128]{1,0:T(1,128)}) custom-call(f32[1024,128]{1,0:T(8,128)} %weight_grad.1.ar, f32[8,128]{1,0:T(8,128)} %get-tuple-element.19.count), custom_call_target="tpu_custom_call" | custom-call | tf_op jit(solution)/shard_map/reduce/pallas_call | solution.py:377
  203.0 1.9 copy.15
  204.8 1.3 copy.16

commit v2 on v1

v2 whole, which is shorter than its diff:
```python
import functools

import jax
import jax.numpy as jnp
from jax import lax
from jax.experimental import pallas as pl
from jax.experimental.pallas import tpu as pltpu
from jax.sharding import PartitionSpec as P

MESH = pl.DeviceIdType.MESH
PEERS = 4
LANES = 128
BLOCK = 256
AR_ROWS = 1024
NT = (((1,), (1,)), ((), ()))
TN = (((0,), (0,)), ((), ()))
F32 = jnp.float32
BF16 = jnp.bfloat16
VMEM = pl.BlockSpec(memory_space=pltpu.VMEM)
SMEM = pl.BlockSpec(memory_space=pltpu.SMEM)
ANY = pl.BlockSpec(memory_space=pl.ANY)


def row_digits(n_rows):
    digits, stride = [], 1
    while stride < n_rows:
        size = min(4, n_rows // stride)
        digits.append((size, stride))
        stride *= size
    return digits


def pieces(value):
    first = value.astype(BF16)
    rest = value - first.astype(F32)
    second = rest.astype(BF16)
    return [first, second, (rest - second.astype(F32)).astype(BF16)]


def iota(shape, dim):
    return lax.broadcasted_iota(jnp.int32, shape, dim)


def block_of_unit(shape):
    return lax.shift_right_logical(iota(shape, 0) * 9363, 16)


def spread_classes(n_class):
    unit = iota((LANES, 8), 0)
    return ((unit - block_of_unit((LANES, 8)) * n_class) == iota((LANES, 8), 1)).astype(F32).astype(BF16)


def block_rows(blk):
    return pl.ds(pl.multiple_of(blk * BLOCK, BLOCK), BLOCK)


def remote(src, dst, send, recv, dev):
    return pltpu.make_async_remote_copy(src_ref=src, dst_ref=dst, send_sem=send, recv_sem=recv,
                                        device_id=dev, device_id_type=MESH)


def finish(copies):
    for copy in copies:
        copy.wait_recv()
    for copy in copies:
        copy.wait_send()


def grid_peers(n_rows, n_cols):
    row, col = lax.axis_index('row'), lax.axis_index('col')
    return [(row, lax.rem(col + n_cols - 1, n_cols)), (row, lax.rem(col + 1, n_cols)),
            (lax.rem(row + n_rows - 1, n_rows), col), (lax.rem(row + 1, n_rows), col)]


def torus_axes(n_rows, n_cols):
    row, col = lax.axis_index('row'), lax.axis_index('col')
    axes = [(n_cols, col, lambda d: (row, lax.rem(col + d, n_cols)))]
    for size, stride in row_digits(n_rows):
        place = lax.rem(row // stride, size)
        axes.append((size, place, functools.partial(
            lambda d, size, stride, place: (row + (lax.rem(place + d, size) - place) * stride, col),
            size=size, stride=stride, place=place)))
    return axes


def arrive(devices):
    for dev in devices:
        pl.semaphore_signal(pltpu.get_barrier_semaphore(), inc=1, device_id=dev, device_id_type=MESH)


def meet(devices):
    pl.semaphore_wait(pltpu.get_barrier_semaphore(), len(devices))


def start_exchange(peers, sbuf, rbuf, send_sem, recv_sem):
    copies = [remote(sbuf.at[q], rbuf.at[q ^ 1], send_sem.at[q], recv_sem.at[q ^ 1], peers[q]) for q in range(PEERS)]
    for copy in copies:
        copy.start()
    return copies


def axis_devices(axes):
    return [dev(d) for size, _, dev in axes for d in range(1, size)]


def exchange_kernel(n_rows, n_cols, sbuf, rbuf, send_sem, recv_sem):
    peers = grid_peers(n_rows, n_cols)
    arrive(peers)
    meet(peers)
    finish(start_exchange(peers, sbuf, rbuf, send_sem, recv_sem))


def first_kernel(n_rows, n_cols, xt, send_v, src_v, msk, rbuf, total_out, src4, sbuf, count, cv, cr,
                 send_sem, recv_sem, c_send, c_recv):
    peers, axes = grid_peers(n_rows, n_cols), torus_axes(n_rows, n_cols)
    everyone = peers + axis_devices(axes)
    arrive(everyone)
    n_feat, n_local = xt.shape
    halo = sbuf.shape[1]
    count[...] = jnp.full(count.shape, jnp.sum(msk[...].astype(F32)), F32)
    src4[...] = src_v[...] * 4
    wanted = [jnp.transpose(jnp.broadcast_to(send_v[q:q + 1, :], (LANES, halo))) for q in range(PEERS)]
    wanted = jnp.concatenate([jnp.concatenate(wanted, axis=0)] * (BLOCK // LANES), axis=1)
    place = iota(wanted.shape, 1)

    def pick(blk, total):
        hot = (place == wanted - blk * BLOCK).astype(F32).astype(BF16)
        return total + lax.dot_general(hot, xt[:, block_rows(blk)], NT, preferred_element_type=F32)

    rows = lax.fori_loop(0, n_local // BLOCK, pick, jnp.zeros((PEERS * halo, n_feat), F32)).astype(BF16)
    for q in range(PEERS):
        sbuf[q, :, 0:n_feat] = rows[q * halo:(q + 1) * halo, :]
        sbuf[q, :, n_feat:] = jnp.zeros((halo, sbuf.shape[2] - n_feat), BF16)
    meet(everyone)
    copies = start_exchange(peers, sbuf, rbuf, send_sem, recv_sem)
    for i, (size, _, dev) in enumerate(axes):
        held = count if i == 0 else cv.at[i - 1]
        counts = [remote(held, cr.at[i, d - 1], c_send.at[i, d - 1], c_recv.at[i, d - 1], dev(d))
                  for d in range(1, size)]
        for copy in counts:
            copy.start()
        finish(counts)
        total = held[...]
        for d in range(1, size):
            total = total + cr[i, d - 1]
        cv[i] = total
    total_out[...] = cv[len(axes) - 1]
    finish(copies)


def reduce_over_devices(axes, ar, part, gb, rs, r_send, r_recv, g_send, g_recv):
    length, base, spans, at, offset, held = AR_ROWS, 0, [], 0, 0, ar
    for i, (size, place, dev) in enumerate(axes):
        length //= size
        copies = []
        for d in range(1, size):
            there = pl.multiple_of(lax.rem(place + d, size) * length, 8)
            copies.append(remote(held.at[pl.ds(there, length), :], rs.at[pl.ds(at + (d - 1) * length, length), :],
                                 r_send.at[i, d - 1], r_recv.at[i, d - 1], dev(d)))
        for copy in copies:
            copy.start()
        finish(copies)
        total = held[pl.ds(pl.multiple_of(place * length, 8), length), :]
        for d in range(1, size):
            total = total + rs[at + (d - 1) * length:at + d * length, :]
        part[offset:offset + length, :] = total
        held = part.at[pl.ds(offset, length), :]
        base = pl.multiple_of(base + place * length, 8)
        at += (size - 1) * length
        offset += length
        spans.append((base, length))
    gb[pl.ds(base, length), :] = held[...]
    for i in reversed(range(len(axes))):
        size, _, dev = axes[i]
        base, length = spans[i]
        here = gb.at[pl.ds(base, length), :]
        copies = [remote(here, here, g_send.at[i, d - 1], g_recv.at[i, d - 1], dev(d)) for d in range(1, size)]
        for copy in copies:
            copy.start()
        finish(copies)


def turn_weights(wt_v, wcol):
    degree, n_local = wt_v.shape

    def turn(blk, _):
        at = pl.ds(pl.multiple_of(blk * LANES, LANES), LANES)
        wcol[at, :] = jnp.transpose(jnp.concatenate([wt_v[:, at], jnp.zeros((8 - degree, LANES), F32)], axis=0))
        return 0

    lax.fori_loop(0, n_local // LANES, turn, 0)


def store_halo(table, n_local, rbuf):
    halo = rbuf.shape[1]
    for p in range(PEERS):
        for j in range(rbuf.shape[2] // LANES):
            table[pl.ds((n_local + p * halo) * 4 + j, halo, stride=4), :] = (
                rbuf[p, :, j * LANES:(j + 1) * LANES].astype(F32))


GROUP = 16


def spread_weights(wcol, spread, first):
    some = wcol[pl.ds(pl.multiple_of(first, GROUP), GROUP), :]
    for k in range(spread.shape[0]):
        spread[k] = jnp.broadcast_to(some[:, k:k + 1], (GROUP, LANES))


def gather_block(table, parts, src_s, wcol, spreads, zb, blk):
    degree, n_local = src_s.shape

    def some(i, _):
        for half in range(2):
            local = i * (2 * GROUP) + half * GROUP
            base = blk * BLOCK + local
            for s in range(GROUP):
                total = None
                for k in range(degree):
                    at = pl.multiple_of(src_s[k, base + s], 4)
                    weight = jnp.broadcast_to(spreads[half][k, s:s + 1, :], (parts, LANES))
                    term = table[pl.ds(at, parts), :] * weight
                    total = term if total is None else total + term
                zb[pl.ds(pl.multiple_of((local + s) * parts, parts), parts), :] = total
            spread_weights(wcol, spreads[1 - half], jnp.minimum(base + GROUP, n_local - GROUP) if half else base + GROUP)
        return 0

    lax.fori_loop(0, BLOCK // (2 * GROUP), some, 0)
    return jnp.concatenate([zb[pl.ds(j, BLOCK, stride=parts), :] for j in range(parts)], axis=1).astype(BF16)


def layer_one_kernel(src4, send_s, xt, wt_v, rbuf, w1, z1, h1, sbuf,
                     src_s, tab, tab2, wcol, spread_a, spread_b, zb, w1b, z1_v, h1_v, sem):
    n_feat, n_local = xt.shape
    n_blocks = n_local // BLOCK
    halo = sbuf.shape[1]
    indices = pltpu.make_async_copy(src4, src_s, sem.at[0])
    indices.start()
    eye = (iota((BLOCK, BLOCK), 0) == iota((BLOCK, BLOCK), 1)).astype(F32).astype(BF16)

    def fill_table(blk, _):
        rows = lax.dot_general(eye, xt[:, block_rows(blk)], NT, preferred_element_type=F32)
        for j in range(4):
            part = rows[:, j * LANES:(j + 1) * LANES]
            if part.shape[1] < LANES:
                part = jnp.concatenate([part, jnp.zeros((BLOCK, LANES - part.shape[1]), F32)], axis=1)
            tab[pl.ds(blk * (4 * BLOCK) + j, BLOCK, stride=4), :] = part
        return 0

    lax.fori_loop(0, n_blocks, fill_table, 0)
    turn_weights(wt_v, wcol)
    w1b[...] = jnp.zeros(w1b.shape, BF16)
    w1b[0:n_feat, :] = w1[...].astype(BF16)
    store_halo(tab, n_local, rbuf)
    spread_weights(wcol, spread_a, 0)
    indices.wait()

    def layer_one(blk, _):
        rows = block_rows(blk)
        z = gather_block(tab, 4, src_s, wcol, (spread_a, spread_b), zb, blk)
        z1_v[rows, :] = z
        h = jnp.maximum(jnp.dot(z, w1b[...], preferred_element_type=F32), 0.0).astype(BF16)
        h1_v[rows, :] = h
        pltpu.make_async_copy(z1_v.at[rows, :], z1.at[rows, :], sem.at[1]).start()
        pltpu.make_async_copy(h1_v.at[rows, :], h1.at[rows, :], sem.at[2]).start()
        for j in range(2):
            tab2[pl.ds(blk * (2 * BLOCK) + j, BLOCK, stride=2), :] = h[:, j * LANES:(j + 1) * LANES].astype(F32)
        return 0

    lax.fori_loop(0, n_blocks, layer_one, 0)

    for q in range(PEERS):
        def take(i, _):
            for s in range(16):
                r = i * 16 + s
                at = pl.multiple_of(send_s[q, r] * 2, 2)
                zb[pl.ds(pl.multiple_of(r * 2, 2), 2), :] = tab2[pl.ds(at, 2), :]
            return 0
        lax.fori_loop(0, halo // 16, take, 0)
        for j in range(2):
            sbuf[q, :, j * LANES:(j + 1) * LANES] = zb[pl.ds(j, halo, stride=2), :].astype(BF16)
    pltpu.make_async_copy(z1_v, z1, sem.at[1]).wait()
    pltpu.make_async_copy(h1_v, h1, sem.at[2]).wait()


def layer_two_kernel(src4, wt_v, h1, rbuf, w2t, z2, lg, src_s, tab, wcol, spread_a, spread_b, zb, sem):
    n_class = w2t.shape[0]
    n_local = h1.shape[0]
    n_blocks = n_local // BLOCK
    indices = pltpu.make_async_copy(src4, src_s, sem)
    indices.start()

    def fill_table(blk, _):
        rows = h1[block_rows(blk), :].astype(F32)
        for j in range(2):
            tab[pl.ds(blk * (4 * BLOCK) + j, BLOCK, stride=4), :] = rows[:, j * LANES:(j + 1) * LANES]
        return 0

    lax.fori_loop(0, n_blocks, fill_table, 0)
    turn_weights(wt_v, wcol)
    store_halo(tab, n_local, rbuf)
    spread_weights(wcol, spread_a, 0)
    w2p = jnp.concatenate([w2t[...], jnp.zeros((8 - n_class, w2t.shape[1]), F32)], axis=0).astype(BF16)
    indices.wait()

    def layer_two(blk, _):
        rows = block_rows(blk)
        z = gather_block(tab, 2, src_s, wcol, (spread_a, spread_b), zb, blk)
        z2[rows, :] = z
        lg[:, rows] = lax.dot_general(w2p, z, NT, preferred_element_type=F32)
        return 0

    lax.fori_loop(0, n_blocks, layer_two, 0)


def last_kernel(n_rows, n_cols, n_feat, src_v, wt_v, lab, msk, count, logit, z2, w2t, send_v, z1, h1,
                g1_out, g2_out, loss_out, z1_v, h1_v, lg, acc, g2t, hs, hr, ar, part_sum, gb, rs,
                sem, send_sem, recv_sem, r_send, r_recv, g_send, g_recv):
    peers, axes = grid_peers(n_rows, n_cols), torus_axes(n_rows, n_cols)
    everyone = peers + axis_devices(axes)
    arrive(everyone)
    z1_load = pltpu.make_async_copy(z1, z1_v, sem.at[0])
    h1_load = pltpu.make_async_copy(h1, h1_v, sem.at[1])
    z1_load.start()
    h1_load.start()
    degree, n_local = src_v.shape
    n_class = w2t.shape[0]
    n_blocks = n_local // BLOCK
    halo = hs.shape[2]
    half = AR_ROWS // 2

    logits = logit[...]
    cls = iota(logits.shape, 0)
    real = cls < n_class
    top = jnp.max(jnp.where(real, logits, jnp.finfo(F32).min), axis=0, keepdims=True)
    log_norm = top + jnp.log(jnp.sum(jnp.where(real, jnp.exp(logits - top), 0.0), axis=0, keepdims=True))
    onehot = (cls == lab[...]).astype(F32)
    picked = jnp.sum(onehot * logits, axis=0, keepdims=True)
    weight = msk[...].astype(F32)
    loss_sum = jnp.sum(weight * (log_norm - picked), axis=1, keepdims=True)
    prob = jnp.where(real, jnp.exp(logits - log_norm), 0.0)
    lg[...] = (prob - onehot) * (weight / count[0:1, 0:1])

    spread_cls = spread_classes(n_class)
    lc_blk = block_of_unit((LANES, BLOCK))
    slot = iota((BLOCK, BLOCK), 0)
    acc[...] = jnp.zeros(acc.shape, F32)
    g2t[...] = jnp.zeros(g2t.shape, F32)

    def scatter(blk, _):
        cols = block_rows(blk)
        g = lg[:, cols].astype(BF16)
        g2t[...] += jnp.dot(g, z2[cols, :], preferred_element_type=F32)
        tiled = jnp.dot(spread_cls, g, preferred_element_type=F32)
        total = acc[...]
        for k in range(degree):
            src = src_v[k:k + 1, cols]
            left = jnp.where(lax.shift_right_logical(src, 8) == lc_blk, tiled, 0.0).astype(BF16)
            here = (src & (BLOCK - 1)) == slot
            for part in pieces(wt_v[k:k + 1, cols]):
                right = jnp.where(here, part.astype(F32), 0.0).astype(BF16)
                total = total + lax.dot_general(left, right, NT, preferred_element_type=F32)
        acc[...] = total
        return 0

    lax.fori_loop(0, n_blocks, scatter, 0)

    hs[...] = jnp.zeros(hs.shape, F32)
    for p in range(PEERS):
        first = (n_local + p * halo) // BLOCK * n_class
        lane = (n_local + p * halo) % BLOCK
        hs[p, 0:n_class, :] = acc[first:first + n_class, lane:lane + halo]
    meet(everyone)
    copies = start_exchange(peers, hs, hr, send_sem, recv_sem)

    w2p = jnp.concatenate([w2t[...], jnp.zeros((8 - n_class, w2t.shape[1]), F32)], axis=0).astype(BF16)
    w2_tiled = jnp.dot(spread_cls, w2p, preferred_element_type=F32)
    ar[...] = jnp.zeros(ar.shape, F32)
    dst = send_v[...]
    wide = dst.shape[1]
    dst_blk = lax.shift_right_logical(dst, 8) == block_of_unit((LANES, wide))
    right = ((dst & (BLOCK - 1)) == iota((BLOCK, wide), 0)).astype(F32).astype(BF16)
    z1_load.wait()
    h1_load.wait()
    finish(copies)

    total = acc[...]
    returned = jnp.concatenate([hr[q] for q in range(PEERS)], axis=1)
    for part in pieces(returned):
        tiled = jnp.dot(spread_cls, part, preferred_element_type=F32)
        left = jnp.where(dst_blk, tiled, 0.0).astype(BF16)
        total = total + lax.dot_general(left, right, NT, preferred_element_type=F32)
    turned = jnp.concatenate(pieces(jnp.transpose(total)), axis=1)

    def weight_grad(blk, _):
        rows = block_rows(blk)
        w2_here = jnp.where(lc_blk == blk, w2_tiled, 0.0).astype(BF16)
        dh = jnp.dot(turned, jnp.concatenate([w2_here] * 3, axis=0), preferred_element_type=F32)
        d_one = jnp.where(h1_v[rows, :].astype(F32) > 0, dh, 0.0).astype(BF16)
        grad = lax.dot_general(z1_v[rows, :], d_one, TN, preferred_element_type=F32)
        ar[0:half, :] += grad[:, :LANES]
        ar[half:2 * half, :] += grad[:, LANES:]
        return 0

    lax.fori_loop(0, n_blocks, weight_grad, 0)
    for j in range(2):
        ar[j * half + n_feat:j * half + n_feat + n_class, :] = g2t[0:n_class, j * LANES:(j + 1) * LANES]
    ar[n_feat + n_class:n_feat + n_class + 1, :] = jnp.broadcast_to(loss_sum, (1, LANES))

    reduce_over_devices(axes, ar, part_sum, gb, rs, r_send, r_recv, g_send, g_recv)
    for j in range(2):
        lanes = slice(j * LANES, (j + 1) * LANES)
        g1_out[:, lanes] = gb[j * half:j * half + n_feat, :]
        g2_out[:, lanes] = gb[j * half + n_feat:j * half + n_feat + n_class, :]
    loss_out[...] = gb[n_feat + n_class:n_feat + n_class + 1, :] / count[0:1, :]


def call(kernel, name, outs, in_specs, out_specs, scratch, args, collective=None):
    params = dict(vmem_limit_bytes=60 * 1024 * 1024)
    if collective is not None:
        params.update(collective_id=collective, has_side_effects=True)
    shapes = tuple(jax.ShapeDtypeStruct(*o) for o in outs)
    return pl.pallas_call(kernel, out_shape=shapes, in_specs=in_specs, out_specs=tuple(out_specs),
                          scratch_shapes=scratch, compiler_params=pltpu.CompilerParams(**params), name=name)(*args)


def solution(mesh):
    n_rows = mesh.shape['row']
    n_cols = mesh.shape['col']
    grid_axes = ('row', 'col')

    def device_step(node_feat, w_one, w_two, send_rows, edge_src, edge_wt, labels, label_mask):
        n_local, n_feat = node_feat.shape
        hidden, n_class = w_two.shape
        halo = send_rows.shape[1]
        degree = edge_src.shape[1]
        ext = n_local + PEERS * halo
        sizes = [n_cols] + [s for s, _ in row_digits(n_rows)]
        n_axes = len(sizes)
        dma, vm = pltpu.SemaphoreType.DMA, pltpu.VMEM
        feat_pad = 4 * LANES
        xt, src_v, wt_v, w2t = node_feat.T, edge_src.T, edge_wt.T, w_two.T
        lab, msk = labels.reshape(1, -1), label_mask.reshape(1, -1)
        spreads = [vm((degree, GROUP, LANES), F32)] * 2

        rbuf, count, src4 = call(
            functools.partial(first_kernel, n_rows, n_cols), 'first',
            [((PEERS, halo, feat_pad), BF16), ((8, LANES), F32), ((degree, n_local), jnp.int32)],
            [VMEM] * 4, [VMEM] * 3,
            [vm((PEERS, halo, feat_pad), BF16), vm((8, LANES), F32),
             vm((n_axes, 8, LANES), F32), vm((n_axes, 3, 8, LANES), F32),
             dma((PEERS,)), dma((PEERS,)), dma((n_axes, 3)), dma((n_axes, 3))], (xt, send_rows, src_v, msk), 0)
        z1, h1, sbuf2 = call(
            layer_one_kernel, 'layer_one',
            [((n_local, feat_pad), BF16), ((n_local, hidden), BF16), ((PEERS, halo, hidden), BF16)],
            [ANY, SMEM] + [VMEM] * 4, [ANY, ANY, VMEM],
            [pltpu.SMEM((degree, n_local), jnp.int32), vm((ext * 4, LANES), F32), vm((n_local * 2, LANES), F32),
             vm((n_local, 8), F32), *spreads, vm((BLOCK * 4, LANES), F32), vm((feat_pad, hidden), BF16),
             vm((n_local, feat_pad), BF16), vm((n_local, hidden), BF16), dma((3,))],
            (src4, send_rows, xt, wt_v, rbuf, w_one))
        rbuf2, = call(functools.partial(exchange_kernel, n_rows, n_cols), 'exchange_hidden',
                      [((PEERS, halo, hidden), BF16)], [VMEM], [VMEM], [dma((PEERS,)), dma((PEERS,))], (sbuf2,), 1)
        z2, logit = call(
            layer_two_kernel, 'layer_two', [((n_local, hidden), BF16), ((8, n_local), F32)],
            [ANY] + [VMEM] * 4, [VMEM] * 2,
            [pltpu.SMEM((degree, n_local), jnp.int32), vm((ext * 4, LANES), F32), vm((n_local, 8), F32), *spreads,
             vm((BLOCK * 2, LANES), F32), dma(())],
            (src4, wt_v, h1, rbuf2, w2t))
        part_rows, rs_rows, left = 0, 0, AR_ROWS
        for size in sizes:
            left //= size
            part_rows += left
            rs_rows += (size - 1) * left
        g1, g2, total = call(
            functools.partial(last_kernel, n_rows, n_cols, n_feat), 'last',
            [((n_feat, hidden), F32), ((n_class, hidden), F32), ((1, LANES), F32)],
            [VMEM] * 9 + [ANY] * 2, [VMEM] * 3,
            [vm((n_local, feat_pad), BF16), vm((n_local, hidden), BF16), vm((8, n_local), F32),
             vm((LANES, BLOCK), F32), vm((8, hidden), F32), vm((PEERS, 8, halo), F32), vm((PEERS, 8, halo), F32),
             vm((AR_ROWS, LANES), F32), vm((part_rows, LANES), F32), vm((AR_ROWS, LANES), F32),
             vm((rs_rows, LANES), F32), dma((2,)), dma((PEERS,)), dma((PEERS,)),
             dma((n_axes, 3)), dma((n_axes, 3)), dma((n_axes, 3)), dma((n_axes, 3))],
            (src_v, wt_v, lab, msk, count, logit, z2, w2t, send_rows.reshape(1, -1), z1, h1), 2)
        return total[0, 0], g1, g2.T

    rows_spec = P(grid_axes, None)
    vec_spec = P(grid_axes)
    return jax.shard_map(device_step, mesh=mesh,
                         in_specs=(rows_spec, P(), P(), rows_spec, rows_spec, rows_spec, vec_spec, vec_spec),
                         out_specs=(P(), P(), P()), check_vma=False)
```

time: 208 us -> 234 us (1.12)
  Pallas kernels: 199 us -> 228 us
    pallas_call x8 -> x5, Pallas kernels: 199 us -> 228 us  [call(): pl.pallas_call(kernel, out_shape=shapes, in_specs=in_specs, out_specs=tup...]
where the time goes in v2:
time: 234 us
  Pallas kernels  228 us (97%)
  local copies, waits for them, and re-layouts  3.15 us (1%)
  between operations  2.36 us (1%)
    pallas_call x5, Pallas kernels, call(): pl.pallas_call(kernel, out_shape=shapes, in_specs=in_specs, out_specs=tup...  228 us

profile of v2, /device:TPU:1, one launch (start us, length us, event | category | flops | bytes accessed | tf_op | source)
XLA Modules:
  0.0 233.9 jit_solution(2595047236635871257)
XLA Ops:
  0.6 26.4 %first.1 = (bf16[4,128,512]{2,1,0:T(8,128)(2,1)}, f32[8,128]{1,0:T(8,128)}, s32[6,4096]{1,0:T(8,128)}) custom-call(bf16[500,4096]{1,0:T(8,128)(2,1)} %bitcast.10, s32[4,128]{1,0:T(4,128)} %send_s.1, s32[6,4096]{1,0:T(8,128)} %bitcast.15, s32[1,4096]{1,0:T(1,128)} %bitcast.17), custom_call_target="tpu_custom_call" | custom-call | tf_op jit(solution)/shard_map/first/pallas_call | solution.py:424
  27.1 67.3 %layer_one.1 = (bf16[4096,512]{1,0:T(8,128)(2,1)}, bf16[4096,256]{1,0:T(8,128)(2,1)}, bf16[4,128,256]{2,1,0:T(8,128)(2,1)}) custom-call(s32[6,4096]{1,0:T(8,128)} %get-tuple-element.15.src4, s32[4,128]{1,0:T(4,128)} %send_s.1, bf16[500,4096]{1,0:T(8,128)(2,1)} %bitcast.11, f32[6,4096]{1,0:T(8,128)} %bitcast.12, bf16[4,128,512]{2,1,0:T(8,128)(2,1)} %get-tuple-element.16.rbuf, ...), custom_call_target="tpu_custom_call" | custom-call | tf_op jit(solution)/shard_map/layer_one/pallas_call | solution.py:424
  94.4 10.3 %exchange_hidden.1.rbuf = bf16[4,128,256]{2,1,0:T(8,128)(2,1)} custom-call(bf16[4,128,256]{2,1,0:T(8,128)(2,1)} %get-tuple-element.18.sbuf), custom_call_target="tpu_custom_call" | custom-call | tf_op jit(solution)/shard_map/exchange_hidden/pallas_call | solution.py:424
  104.7 61.0 %layer_two.1 = (bf16[4096,256]{1,0:T(8,128)(2,1)}, f32[8,4096]{1,0:T(8,128)}) custom-call(s32[6,4096]{1,0:T(8,128)} %get-tuple-element.15.src4, f32[6,4096]{1,0:T(8,128)} %bitcast.13, bf16[4096,256]{1,0:T(8,128)(2,1)} %get-tuple-element.17.h1, bf16[4,128,256]{2,1,0:T(8,128)(2,1)} %exchange_hidden.1.rbuf, f32[7,256]{1,0:T(8,128)} %bitcast.19), custom_call_target="tpu_custom_call" | custom-call | tf_op jit(solution)/shard_map/layer_two/pallas_call | solution.py:424
  165.7 63.3 %last.1 = (f32[500,256]{1,0:T(8,128)}, f32[7,256]{1,0:T(8,128)}, f32[1,128]{1,0:T(1,128)}) custom-call(s32[6,4096]{1,0:T(8,128)} %bitcast.16, f32[6,4096]{1,0:T(8,128)} %bitcast.14, s32[1,4096]{1,0:T(1,128)} %bitcast.22, s32[1,4096]{1,0:T(1,128)} %bitcast.18, f32[8,128]{1,0:T(8,128)} %get-tuple-element.14.count, f32[8,4096]{1,0:T(8,128)} %get-tuple-element.19.logit, ...), custom_call_target="tpu_custom_call" | custom-call | tf_op jit(solution)/shard_map/last/pallas_call | solution.py:424
  229.6 1.9 copy.15
  231.5 1.3 copy.16

commit v3 on v2

--- a/solution.py
+++ b/solution.py
@@ -118,7 +118,10 @@
     n_feat, n_local = xt.shape
     halo = sbuf.shape[1]
     count[...] = jnp.full(count.shape, jnp.sum(msk[...].astype(F32)), F32)
-    src4[...] = src_v[...] * 4
+    degree = src_v.shape[0]
+    for b in range(n_local // LANES):
+        src4[b, 0:degree, :] = src_v[:, b * LANES:(b + 1) * LANES] * 4
+        src4[b, degree:, :] = jnp.zeros((src4.shape[1] - degree, LANES), jnp.int32)
     wanted = [jnp.transpose(jnp.broadcast_to(send_v[q:q + 1, :], (LANES, halo))) for q in range(PEERS)]
     wanted = jnp.concatenate([jnp.concatenate(wanted, axis=0)] * (BLOCK // LANES), axis=1)
     place = iota(wanted.shape, 1)
@@ -180,15 +183,17 @@
         finish(copies)
 
 
-def turn_weights(wt_v, wcol):
+def spread_weights(wt_v, wb):
     degree, n_local = wt_v.shape
 
-    def turn(blk, _):
-        at = pl.ds(pl.multiple_of(blk * LANES, LANES), LANES)
-        wcol[at, :] = jnp.transpose(jnp.concatenate([wt_v[:, at], jnp.zeros((8 - degree, LANES), F32)], axis=0))
-        return 0
-
-    lax.fori_loop(0, n_local // LANES, turn, 0)
+    def spread(blk, _):
+        for half in range(2):
+            at = pl.ds(pl.multiple_of(blk * (2 * LANES) + half * LANES, LANES), LANES)
+            for k in range(degree):
+                wb[k, at, :] = jnp.transpose(jnp.broadcast_to(wt_v[k:k + 1, at], (LANES, LANES)))
+        return 0
+
+    lax.fori_loop(0, n_local // (2 * LANES), spread, 0)
 
 
 def store_halo(table, n_local, rbuf):
@@ -202,36 +207,28 @@
 GROUP = 16
 
 
-def spread_weights(wcol, spread, first):
-    some = wcol[pl.ds(pl.multiple_of(first, GROUP), GROUP), :]
-    for k in range(spread.shape[0]):
-        spread[k] = jnp.broadcast_to(some[:, k:k + 1], (GROUP, LANES))
-
-
-def gather_block(table, parts, src_s, wcol, spreads, zb, blk):
-    degree, n_local = src_s.shape
+def gather_block(table, parts, src_s, wb, zb, blk):
+    degree = wb.shape[0]
 
     def some(i, _):
-        for half in range(2):
-            local = i * (2 * GROUP) + half * GROUP
-            base = blk * BLOCK + local
-            for s in range(GROUP):
-                total = None
-                for k in range(degree):
-                    at = pl.multiple_of(src_s[k, base + s], 4)
-                    weight = jnp.broadcast_to(spreads[half][k, s:s + 1, :], (parts, LANES))
-                    term = table[pl.ds(at, parts), :] * weight
-                    total = term if total is None else total + term
-                zb[pl.ds(pl.multiple_of((local + s) * parts, parts), parts), :] = total
-            spread_weights(wcol, spreads[1 - half], jnp.minimum(base + GROUP, n_local - GROUP) if half else base + GROUP)
-        return 0
-
-    lax.fori_loop(0, BLOCK // (2 * GROUP), some, 0)
+        local = i * GROUP
+        base = blk * BLOCK + local
+        word = lax.shift_left(lax.shift_right_logical(base, 7), 10) + (base & (LANES - 1))
+        for s in range(GROUP):
+            total = None
+            for k in range(degree):
+                at = pl.multiple_of(src_s[word + (k * LANES + s)], 4)
+                term = table[pl.ds(at, parts), :] * jnp.broadcast_to(wb[k, pl.ds(base + s, 1), :], (parts, LANES))
+                total = term if total is None else total + term
+            zb[pl.ds(pl.multiple_of((local + s) * parts, parts), parts), :] = total
+        return 0
+
+    lax.fori_loop(0, BLOCK // GROUP, some, 0)
     return jnp.concatenate([zb[pl.ds(j, BLOCK, stride=parts), :] for j in range(parts)], axis=1).astype(BF16)
 
 
 def layer_one_kernel(src4, send_s, xt, wt_v, rbuf, w1, z1, h1, sbuf,
-                     src_s, tab, tab2, wcol, spread_a, spread_b, zb, w1b, z1_v, h1_v, sem):
+                     src_s, tab, tab2, wb, zb, w1b, z1_v, h1_v, sem):
     n_feat, n_local = xt.shape
     n_blocks = n_local // BLOCK
     halo = sbuf.shape[1]
@@ -249,16 +246,15 @@
         return 0
 
     lax.fori_loop(0, n_blocks, fill_table, 0)
-    turn_weights(wt_v, wcol)
+    spread_weights(wt_v, wb)
     w1b[...] = jnp.zeros(w1b.shape, BF16)
     w1b[0:n_feat, :] = w1[...].astype(BF16)
     store_halo(tab, n_local, rbuf)
-    spread_weights(wcol, spread_a, 0)
     indices.wait()
 
     def layer_one(blk, _):
         rows = block_rows(blk)
-        z = gather_block(tab, 4, src_s, wcol, (spread_a, spread_b), zb, blk)
+        z = gather_block(tab, 4, src_s, wb, zb, blk)
         z1_v[rows, :] = z
         h = jnp.maximum(jnp.dot(z, w1b[...], preferred_element_type=F32), 0.0).astype(BF16)
         h1_v[rows, :] = h
@@ -284,7 +280,7 @@
     pltpu.make_async_copy(h1_v, h1, sem.at[2]).wait()
 
 
-def layer_two_kernel(src4, wt_v, h1, rbuf, w2t, z2, lg, src_s, tab, wcol, spread_a, spread_b, zb, sem):
+def layer_two_kernel(src4, wt_v, h1, rbuf, w2t, z2, lg, src_s, tab, wb, zb, sem):
     n_class = w2t.shape[0]
     n_local = h1.shape[0]
     n_blocks = n_local // BLOCK
@@ -298,15 +294,14 @@
         return 0
 
     lax.fori_loop(0, n_blocks, fill_table, 0)
-    turn_weights(wt_v, wcol)
+    spread_weights(wt_v, wb)
     store_halo(tab, n_local, rbuf)
-    spread_weights(wcol, spread_a, 0)
     w2p = jnp.concatenate([w2t[...], jnp.zeros((8 - n_class, w2t.shape[1]), F32)], axis=0).astype(BF16)
     indices.wait()
 
     def layer_two(blk, _):
         rows = block_rows(blk)
-        z = gather_block(tab, 2, src_s, wcol, (spread_a, spread_b), zb, blk)
+        z = gather_block(tab, 2, src_s, wb, zb, blk)
         z2[rows, :] = z
         lg[:, rows] = lax.dot_general(w2p, z, NT, preferred_element_type=F32)
         return 0
@@ -442,21 +437,21 @@
         feat_pad = 4 * LANES
         xt, src_v, wt_v, w2t = node_feat.T, edge_src.T, edge_wt.T, w_two.T
         lab, msk = labels.reshape(1, -1), label_mask.reshape(1, -1)
-        spreads = [vm((degree, GROUP, LANES), F32)] * 2
 
         rbuf, count, src4 = call(
             functools.partial(first_kernel, n_rows, n_cols), 'first',
-            [((PEERS, halo, feat_pad), BF16), ((8, LANES), F32), ((degree, n_local), jnp.int32)],
+            [((PEERS, halo, feat_pad), BF16), ((8, LANES), F32), ((n_local // LANES, 8, LANES), jnp.int32)],
             [VMEM] * 4, [VMEM] * 3,
             [vm((PEERS, halo, feat_pad), BF16), vm((8, LANES), F32),
              vm((n_axes, 8, LANES), F32), vm((n_axes, 3, 8, LANES), F32),
              dma((PEERS,)), dma((PEERS,)), dma((n_axes, 3)), dma((n_axes, 3))], (xt, send_rows, src_v, msk), 0)
+        src4 = src4.reshape(-1)
         z1, h1, sbuf2 = call(
             layer_one_kernel, 'layer_one',
             [((n_local, feat_pad), BF16), ((n_local, hidden), BF16), ((PEERS, halo, hidden), BF16)],
             [ANY, SMEM] + [VMEM] * 4, [ANY, ANY, VMEM],
-            [pltpu.SMEM((degree, n_local), jnp.int32), vm((ext * 4, LANES), F32), vm((n_local * 2, LANES), F32),
-             vm((n_local, 8), F32), *spreads, vm((BLOCK * 4, LANES), F32), vm((feat_pad, hidden), BF16),
+            [pltpu.SMEM((8 * n_local,), jnp.int32), vm((ext * 4, LANES), F32), vm((n_local * 2, LANES), F32),
+             vm((degree, n_local, LANES), F32), vm((BLOCK * 4, LANES), F32), vm((feat_pad, hidden), BF16),
              vm((n_local, feat_pad), BF16), vm((n_local, hidden), BF16), dma((3,))],
             (src4, send_rows, xt, wt_v, rbuf, w_one))
         rbuf2, = call(functools.partial(exchange_kernel, n_rows, n_cols), 'exchange_hidden',
@@ -464,7 +459,7 @@
         z2, logit = call(
             layer_two_kernel, 'layer_two', [((n_local, hidden), BF16), ((8, n_local), F32)],
             [ANY] + [VMEM] * 4, [VMEM] * 2,
-            [pltpu.SMEM((degree, n_local), jnp.int32), vm((ext * 4, LANES), F32), vm((n_local, 8), F32), *spreads,
+            [pltpu.SMEM((8 * n_local,), jnp.int32), vm((ext * 4, LANES), F32), vm((degree, n_local, LANES), F32),
              vm((BLOCK * 2, LANES), F32), dma(())],
             (src4, wt_v, h1, rbuf2, w2t))
         part_rows, rs_rows, left = 0, 0, AR_ROWS

time: 234 us -> 177 us (0.76)
  Pallas kernels: 228 us -> 171 us
    pallas_call x5, Pallas kernels: 228 us -> 171 us  [call(): pl.pallas_call(kernel, out_shape=shapes, in_specs=in_specs, out_specs=tup...]
where the time goes in v3:
time: 177 us
  Pallas kernels  171 us (97%)
  local copies, waits for them, and re-layouts  3.15 us (2%)
  between operations  2.36 us (1%)
    pallas_call x5, Pallas kernels, call(): pl.pallas_call(kernel, out_shape=shapes, in_specs=in_specs, out_specs=tup...  171 us

profile of v3, /device:TPU:1, one launch (start us, length us, event | category | flops | bytes accessed | tf_op | source)
XLA Modules:
  0.0 177.0 jit_solution(9097643874231901933)
XLA Ops:
  0.6 26.4 %first.1 = (bf16[4,128,512]{2,1,0:T(8,128)(2,1)}, f32[8,128]{1,0:T(8,128)}, s32[32,8,128]{2,1,0:T(8,128)}) custom-call(bf16[500,4096]{1,0:T(8,128)(2,1)} %bitcast.11, s32[4,128]{1,0:T(4,128)} %send_s.1, s32[6,4096]{1,0:T(8,128)} %bitcast.16, s32[1,4096]{1,0:T(1,128)} %bitcast.20), custom_call_target="tpu_custom_call" | custom-call | tf_op jit(solution)/shard_map/first/pallas_call | solution.py:419
  27.1 39.1 %layer_one.1 = (bf16[4096,512]{1,0:T(8,128)(2,1)}, bf16[4096,256]{1,0:T(8,128)(2,1)}, bf16[4,128,256]{2,1,0:T(8,128)(2,1)}) custom-call(s32[32768]{0:T(1024)} %bitcast.18, s32[4,128]{1,0:T(4,128)} %send_s.1, bf16[500,4096]{1,0:T(8,128)(2,1)} %bitcast.12, f32[6,4096]{1,0:T(8,128)} %bitcast.13, bf16[4,128,512]{2,1,0:T(8,128)(2,1)} %get-tuple-element.16.rbuf, ...), custom_call_target="tpu_custom_call" | custom-call | tf_op jit(solution)/shard_map/layer_one/pallas_call | solution.py:419
  66.2 10.3 %exchange_hidden.1.rbuf = bf16[4,128,256]{2,1,0:T(8,128)(2,1)} custom-call(bf16[4,128,256]{2,1,0:T(8,128)(2,1)} %get-tuple-element.18.sbuf), custom_call_target="tpu_custom_call" | custom-call | tf_op jit(solution)/shard_map/exchange_hidden/pallas_call | solution.py:419
  76.5 32.4 %layer_two.1 = (bf16[4096,256]{1,0:T(8,128)(2,1)}, f32[8,4096]{1,0:T(8,128)}) custom-call(s32[32768]{0:T(1024)} %bitcast.19, f32[6,4096]{1,0:T(8,128)} %bitcast.14, bf16[4096,256]{1,0:T(8,128)(2,1)} %get-tuple-element.17.h1, bf16[4,128,256]{2,1,0:T(8,128)(2,1)} %exchange_hidden.1.rbuf, f32[7,256]{1,0:T(8,128)} %bitcast.22), custom_call_target="tpu_custom_call" | custom-call | tf_op jit(solution)/shard_map/layer_two/pallas_call | solution.py:419
  108.8 63.3 %last.1 = (f32[500,256]{1,0:T(8,128)}, f32[7,256]{1,0:T(8,128)}, f32[1,128]{1,0:T(1,128)}) custom-call(s32[6,4096]{1,0:T(8,128)} %bitcast.17, f32[6,4096]{1,0:T(8,128)} %bitcast.15, s32[1,4096]{1,0:T(1,128)} %bitcast.25, s32[1,4096]{1,0:T(1,128)} %bitcast.21, f32[8,128]{1,0:T(8,128)} %get-tuple-element.14.count, f32[8,4096]{1,0:T(8,128)} %get-tuple-element.19.logit, ...), custom_call_target="tpu_custom_call" | custom-call | tf_op jit(solution)/shard_map/last/pallas_call | solution.py:419
  172.7 1.9 %copy.15 = f32[500,256]{1,0:T(8,128)} copy(f32[500,256]{1,0:T(8,128)} %get-tuple-element.29) | data formatting | bytes 1024000
  174.5 1.3 copy.16
